TPU v7x, 128 devices: a whole 4x4x4 slice. The times are simulated.
128 devices in a mesh: tm: 16 (over x, y), space: 8 (over z, core).
Axes of the slice: x: 4, y: 4, z: 4, core: 2. Of those that a mesh axis runs over, the one named last changes fastest.
Arguments:
- initial_state: float32 [1024, 1024], P('space'), may hold values from -6 to 6
- guess_coarse: float32 [16, 1024, 1024], P('tm', 'space'), may hold values from -6 to 6
- force_fine: float32 [16, 1024, 1024], P('tm', 'space'), may hold values from -6 to 6
- force_coarse: float32 [16, 1024, 1024], P('tm', 'space'), may hold values from -6 to 6
- eigen_basis: float32 [1024, 1024], replicated, may hold values from -1 to 1, as said below
- eigen_rates: float32 [1024], replicated, may hold values from 0.02 to 4
- carried_correction: float32 [1024, 1024], replicated, may hold values from -6 to 6
Outputs:
- fine_states: float32 [16, 1024, 1024], P('tm', 'space')
- coarse_states: float32 [16, 1024, 1024], P('tm', 'space')
Inputs may be any that keep to these rules, and one draw needn't show every extreme that they name: `eigen_basis`: an orthogonal matrix: its transpose is its inverse up to float32 rounding.
All inputs are finite; a program needn't handle non-finite values.
Results may differ from a plain program's by a relative error of at most 0.00013.
Values sent between devices are 32-bit elements; how exact they have to be, the bound alone decides.
A program may use at most 64 MiB of HBM per device.

v0:
```python
import jax
import jax.numpy as jnp
from jax import lax
from jax.sharding import Mesh
from jax.sharding import PartitionSpec as P

TM = ("tm_0", "tm_1")


exact_mode = lax.Precision.HIGHEST


def passed_along(block, axis, distance):
    devices = range(lax.axis_size(axis))
    route = [(i - distance, i) for i in devices if i - distance in devices]
    return lax.ppermute(block, axis, route)


def neutral_like(array, identity):
    return jax.tree.map(
        lambda a, e: jnp.broadcast_to(jnp.asarray(e, a.dtype), a.shape), array, identity
    )


def prefix_by_axis(array, axes, combine, identity):
    before = start = neutral_like(array, identity)
    subtotal = array
    for axis in reversed(axes):
        peers, place = (lax.axis_size(axis), lax.axis_index(axis))
        pieces = jax.tree.map(lambda part: lax.all_gather(part, axis), subtotal)
        inside, subtotal = (start, start)
        for k in range(peers):
            passed = k < place
            subtotal = combine(subtotal, jax.tree.map(lambda part: part[k], pieces))
            inside = jax.tree.map(lambda new, old: jnp.where(passed, new, old), subtotal, inside)
        before = combine(inside, before)
    return before


def product(left, right):
    return jnp.dot(left, right, preferred_element_type=jnp.float32, precision=exact_mode)


def reaction(field):
    return field + 0.5 * jnp.tanh(field)


def decay_block(eigen_rates, own_rates, factor):
    return 1.0 / (1.0 + factor * (eigen_rates[:, None] + own_rates[None, :]))


def eigen_block(whole, offset, row_count):
    return lax.dynamic_slice_in_dim(whole, offset, row_count, 1)


def to_eigen(field, eigen_basis):
    right = product(field, eigen_basis)
    columns = lax.all_to_all(right, "space", split_axis=1, concat_axis=0, tiled=True)
    return product(eigen_basis.T, columns)


def from_eigen(coeffs, eigen_basis):
    left = product(eigen_basis, coeffs)
    row_block = lax.all_to_all(left, "space", split_axis=0, concat_axis=1, tiled=True)
    return product(row_block, eigen_basis.T)


def on_device(
    initial_state,
    guess_coarse,
    force_fine,
    force_coarse,
    eigen_basis,
    eigen_rates,
    carried_correction,
):
    row_count = initial_state.shape[0]
    offset = lax.axis_index("space") * row_count
    own_rates = lax.dynamic_slice_in_dim(eigen_rates, offset, row_count, 0)
    fine_decay = decay_block(eigen_rates, own_rates, 1.0)
    coarse_decay = decay_block(eigen_rates, own_rates, 2.0)
    carried_block = eigen_block(carried_correction, offset, row_count)
    at_start = lax.axis_index(TM) == 0
    source_fine = force_fine[0]
    source_coarse = force_coarse[0]

    def previous(state):
        arrived = passed_along(state, TM, 1)
        return jnp.where(at_start, initial_state, arrived)

    def propagate(field, source):
        coeffs = fine_decay * to_eigen(reaction(field) + source, eigen_basis)
        return from_eigen(coeffs, eigen_basis)

    relaxed_fine = propagate(previous(guess_coarse[0]), source_fine)
    relaxed_coarse = propagate(relaxed_fine, source_coarse)
    second_fine = propagate(previous(relaxed_coarse), source_fine)
    residual = fine_decay * to_eigen(reaction(second_fine) + source_coarse, eigen_basis)
    residual = residual - to_eigen(relaxed_coarse, eigen_basis)
    residual = residual + jnp.where(at_start, coarse_decay * carried_block, 0.0)

    def combine(earlier, later):
        scaled = jnp.power(coarse_decay, later[1]) * earlier[0]
        return (scaled + later[0], earlier[1] + later[1])

    identity_pair = (jnp.zeros_like(residual), jnp.zeros((), jnp.float32))
    before, unused = prefix_by_axis(
        (residual, jnp.ones((), jnp.float32)), TM, combine, identity_pair
    )
    correction = coarse_decay * before + residual
    coarse_new = relaxed_coarse + from_eigen(correction, eigen_basis)
    fine_new = propagate(previous(coarse_new), source_fine)
    return (fine_new[None], coarse_new[None])


def solution(mesh):
    torus = Mesh(mesh.devices.reshape(4, 4, mesh.shape["space"]), ("tm_0", "tm_1", "space"))
    return jax.shard_map(
        on_device,
        mesh=torus,
        in_specs=(
            P("space", None),
            P(TM, "space", None),
            P(TM, "space", None),
            P(TM, "space", None),
            P(),
            P(),
            P(),
        ),
        out_specs=(P(TM, "space", None), P(TM, "space", None)),
        check_vma=False,
    )
```

profile of v0, /device:TPU:2, one launch (start us, length us, event | category | flops | bytes accessed | tf_op | source)
XLA Modules:
  0.0 383.5 jit_solution(705079258122861600)
XLA Ops:
  10.7 14.4 %collective-permute-done = f32[128,1024]{1,0:T(8,128)S(1)} collective-permute-done((f32[128,1024]{1,0:T(8,128)}, f32[128,1024]{1,0:T(8,128)S(1)}, u32[]{:S(2)}, u32[]{:S(2)}) %collective-permute-start) | collective-permute-done | bytes 524320 | tf_op jit(solution)/shard_map/ppermute | solution.py:16
  25.0 4.8 %convolution_bitcast_fusion.17 = f32[16,8,8,128]{3,2,1,0:T(8,128)S(1)} fusion(f32[1024,1024]{1,0:T(8,128)} %param.11, f32[1,128,1024]{2,1,0:T(8,128)} %param.9, f32[128,1024]{1,0:T(8,128)} %param.7, f32[128,1024]{1,0:T(8,128)S(1)} %collective-permute-done, pred[]{:T(512)S(6)} %eq.3), kind=kOutput, calls=%fused_computation.25 | convolution fusion | flops 1611137024 | bytes 6291457 | tf_op jit(solution)/shard_map/dot_general | solution.py:41
  30.7 5.3 %all-to-all-start = ((f32[128,8,128]{2,0,1:T(8,128)}), f32[128,8,128]{2,0,1:T(8,128)S(1)}, u32[]{:S(2)}, u32[]{:S(2)}) async-start(f32[128,8,128]{2,0,1:T(8,128)} %bitcast.231), calls=%async_computation | async-start | bytes 1048576 | tf_op jit(solution)/shard_map/all_to_all | solution.py:58
  36.1 10.2 %all-to-all-done = f32[128,8,128]{2,0,1:T(8,128)S(1)} async-done(((f32[128,8,128]{2,0,1:T(8,128)}), f32[128,8,128]{2,0,1:T(8,128)S(1)}, u32[]{:S(2)}, u32[]{:S(2)}) %all-to-all-start) | async-done | bytes 524320 | tf_op jit(solution)/shard_map/all_to_all | solution.py:58
  46.3 4.7 %fusion.6 = f32[1024,128]{0,1:T(8,128)S(1)} fusion(f32[1024,128]{1,0:T(8,128)S(1)} %bitcast.232, f32[1024,1024]{1,0:T(8,128)} %param.11, f32[128]{0:T(128)S(1)} %dynamic_slice.6, f32[1024]{0:T(1024)S(1)} %copy-done.7), kind=kOutput, calls=%fused_computation.24 | convolution fusion | flops 1611137024 | bytes 5247488 | tf_op jit(solution)/shard_map/dot_general | solution.py:41
  55.6 13.4 %all_to_all.209 = f32[8,128,128]{1,2,0:T(8,128)S(1)} all-to-all(f32[8,128,128]{1,2,0:T(8,128)S(1)} %bitcast.242), channel_id=1, replica_groups=mesh['tm_0'=4,'tm_1'=4,'space'=8] {'space'}, dimensions={0} | all-to-all | bytes 1048576 | tf_op jit(solution)/shard_map/all_to_all | solution.py:64
  68.9 4.6 %fusion.111 = f32[128,1024]{1,0:T(8,128)S(1)} fusion(f32[128,1024]{0,1:T(8,128)S(1)} %bitcast.236, f32[1024,1024]{1,0:T(8,128)S(1)} %copy-done), kind=kOutput, calls=%fused_computation.155 | convolution fusion | flops 1610612736 | bytes 5242880 | tf_op jit(solution)/shard_map/dot_general | solution.py:41
  76.0 12.8 %all_to_all.210 = f32[128,8,128]{2,0,1:T(8,128)S(1)} all-to-all(f32[128,8,128]{2,0,1:T(8,128)S(1)} %bitcast.243), channel_id=1, replica_groups=mesh['tm_0'=4,'tm_1'=4,'space'=8] {'space'}, dimensions={1} | all-to-all | bytes 1048576 | tf_op jit(solution)/shard_map/all_to_all | solution.py:58
  91.3 4.5 %convolution_bitcast_fusion.12 = f32[16,8,8,128]{3,2,1,0:T(8,128)S(1)} fusion(f32[1024,128]{0,1:T(8,128)S(1)} %fusion.5, f32[1024,1024]{1,0:T(8,128)S(1)} %copy-done), kind=kOutput, calls=%fused_computation.18 | convolution fusion | flops 1610612736 | bytes 5242880 | tf_op jit(solution)/shard_map/dot_general | solution.py:41
  95.8 13.1 %all_to_all.211 = f32[8,128,128]{1,2,0:T(8,128)S(1)} all-to-all(f32[8,128,128]{1,2,0:T(8,128)S(1)} %bitcast.244), channel_id=1, replica_groups=mesh['tm_0'=4,'tm_1'=4,'space'=8] {'space'}, dimensions={0} | all-to-all | bytes 1048576 | tf_op jit(solution)/shard_map/all_to_all | solution.py:64
  108.9 4.6 %fusion.112 = f32[128,1024]{1,0:T(8,128)S(1)} fusion(f32[128,1024]{0,1:T(8,128)S(1)} %bitcast.238, f32[1024,1024]{1,0:T(8,128)S(1)} %copy-done), kind=kOutput, calls=%fused_computation.156 | convolution fusion | flops 1610612736 | bytes 5242880 | tf_op jit(solution)/shard_map/dot_general | solution.py:41
  115.4 15.4 %collective-permute-done.1 = f32[128,1024]{1,0:T(8,128)S(1)} collective-permute-done((f32[128,1024]{1,0:T(8,128)S(1)}, f32[128,1024]{1,0:T(8,128)S(1)}, u32[]{:S(2)}, u32[]{:S(2)}) %collective-permute-start.1) | collective-permute-done | bytes 524320 | tf_op jit(solution)/shard_map/ppermute | solution.py:16
  133.2 12.8 %all_to_all.212 = f32[128,8,128]{2,0,1:T(8,128)S(1)} all-to-all(f32[128,8,128]{2,0,1:T(8,128)S(1)} %bitcast.245), channel_id=1, replica_groups=mesh['tm_0'=4,'tm_1'=4,'space'=8] {'space'}, dimensions={1} | all-to-all | bytes 1048576 | tf_op jit(solution)/shard_map/all_to_all | solution.py:58
  153.0 12.8 %all_to_all.213 = f32[8,128,128]{1,2,0:T(8,128)S(1)} all-to-all(f32[8,128,128]{1,2,0:T(8,128)S(1)} %bitcast.246), channel_id=1, replica_groups=mesh['tm_0'=4,'tm_1'=4,'space'=8] {'space'}, dimensions={0} | all-to-all | bytes 1048576 | tf_op jit(solution)/shard_map/all_to_all | solution.py:64
  165.8 4.6 %fusion.113 = f32[128,1024]{1,0:T(8,128)S(1)} fusion(f32[128,1024]{0,1:T(8,128)S(1)} %bitcast.240, f32[1024,1024]{1,0:T(8,128)S(1)} %copy-done), kind=kOutput, calls=%fused_computation.157 | convolution fusion | flops 1610612736 | bytes 5242880 | tf_op jit(solution)/shard_map/dot_general | solution.py:41
  177.5 4.6 %convolution_bitcast_fusion.6 = f32[16,8,8,128]{3,2,1,0:T(8,128)S(1)} fusion(f32[128,1024]{1,0:T(8,128)S(1)} %fusion.112, f32[1024,1024]{1,0:T(8,128)} %param.11), kind=kOutput, calls=%fused_computation.10 | convolution fusion | flops 1610612736 | bytes 5242880 | tf_op jit(solution)/shard_map/dot_general | solution.py:41
  182.9 4.8 %all-to-all-done.6 = f32[128,8,128]{2,0,1:T(8,128)S(1)} async-done(((f32[128,8,128]{2,0,1:T(8,128)}), f32[128,8,128]{2,0,1:T(8,128)S(1)}, u32[]{:S(2)}, u32[]{:S(2)}) %all-to-all-start.6) | async-done | bytes 524320 | tf_op jit(solution)/shard_map/all_to_all | solution.py:58
  193.4 4.6 %fusion.3 = f32[1024,128]{0,1:T(8,128)S(1)} fusion(f32[1024,128]{1,0:T(8,128)S(1)} %bitcast.233, f32[1024,1024]{1,0:T(8,128)} %param.11, f32[128]{0:T(128)S(1)} %dynamic_slice.6, f32[1024]{0:T(1024)S(1)} %copy-done.7), kind=kOutput, calls=%fused_computation.12 | convolution fusion | flops 1611137024 | bytes 5247488 | tf_op jit(solution)/shard_map/dot_general | solution.py:41
  201.5 5.6 %fusion.2 = f32[1024,128]{0,1:T(8,128)} fusion(f32[1024,128]{0,1:T(8,128)S(1)} %fusion.3, f32[1024,128]{1,0:T(8,128)S(1)} %bitcast.234, f32[1024,1024]{1,0:T(8,128)} %param.11, f32[1024,128]{0,1:T(8,128)} %copy.39, f32[128]{0:T(128)S(1)} %dynamic_slice.6, f32[1024]{0:T(1024)S(1)} %copy-done.7, pred[]{:T(512)S(6)} %eq.3), kind=kOutput, calls=%fused_computation.9 | convolution fusion | flops 1611661312 | bytes 6296065 | tf_op jit(solution)/shard_map/dot_general | solution.py:41
  208.5 7.7 %all-reduce = f32[4]{0:T(128)S(1)} all-reduce(f32[4]{0:T(128)S(1)} %dynamic-update-slice), channel_id=1, replica_groups=mesh['tm_0'=4,'tm_1'=4,'space'=8] {'tm_1'}, use_global_device_ids=true, to_apply=%add | all-reduce | flops 4 | bytes 32
  216.9 18.0 %all-gather.6.cloned.1.call-done = f32[4096,128]{0,1:T(8,128)} async-done(((f32[1024,128]{0,1:T(8,128)}), f32[4096,128]{0,1:T(8,128)}) %all-gather.6.cloned.1.call-update) | async-done | bytes 2097168 | tf_op jit(solution)/shard_map/all_gather | solution.py:30
  234.9 6.7 %bitcast_add_fusion.4 = f32[1,1024,128]{1,2,0:T(8,128)S(1)} fusion(f32[4096,128]{0,1:T(8,128)} %all-gather.6.cloned.1.call-done, f32[]{:T(128)} %bitcast.16, f32[]{:T(128)} %bitcast.17, f32[]{:T(128)} %bitcast.18, f32[]{:T(128)} %bitcast.19, f32[128]{0:T(128)S(1)} %dynamic_slice.6, f32[1024]{0:T(1024)S(1)} %copy-done.7), kind=kLoop, calls=%fused_computation.51 | loop fusion | flops 1572864 | bytes 2626064 | tf_op jit(solution)/shard_map/add | solution.py:104
  246.4 8.7 %all-reduce.1 = f32[4]{0:T(128)S(1)} all-reduce(f32[4]{0:T(128)S(1)} %dynamic-update-slice.1), channel_id=1, replica_groups=mesh['tm_0'=4,'tm_1'=4,'space'=8] {'tm_0'}, use_global_device_ids=true, to_apply=%add.1 | all-reduce | flops 4 | bytes 32
  256.5 16.0 %all-gather.4.cloned.1.call-done = f32[4,1024,128]{2,1,0:T(8,128)} async-done(((f32[1,1024,128]{2,1,0:T(8,128)}), f32[4,1024,128]{2,1,0:T(8,128)}) %all-gather.4.cloned.1.call-update) | async-done | bytes 2097168 | tf_op jit(solution)/shard_map/all_gather | solution.py:30
  280.5 18.5 %convolution_bitcast_fusion.4 = f32[16,8,8,128]{3,2,1,0:T(8,128)S(1)} fusion(f32[1024,1024]{1,0:T(8,128)} %param.11, f32[1024,128]{0,1:T(8,128)S(1)} %copy-done.4, f32[1,1024,128]{1,2,0:T(8,128)S(1)} %copy.43, f32[1,1024,128]{1,2,0:T(8,128)} %copy.42, f32[1,1024,128]{1,2,0:T(8,128)} %copy.41, f32[1,1024,128]{1,2,0:T(8,128)} %copy.40, ...), kind=kOutput, calls=%fused_computation.6 | convolution fusion | flops 1614807040 | bytes 9441836 | tf_op jit(solution)/shard_map/dot_general | solution.py:41
  299.0 14.8 %all_to_all.214 = f32[8,128,128]{1,2,0:T(8,128)S(1)} all-to-all(f32[8,128,128]{1,2,0:T(8,128)S(1)} %bitcast.247), channel_id=1, replica_groups=mesh['tm_0'=4,'tm_1'=4,'space'=8] {'space'}, dimensions={0} | all-to-all | bytes 1048576 | tf_op jit(solution)/shard_map/all_to_all | solution.py:64
  313.8 4.6 %convolution_add_fusion = f32[128,1024]{1,0:T(8,128)S(1)} fusion(f32[128,1024]{1,0:T(8,128)S(1)} %fusion.112, f32[128,1024]{0,1:T(8,128)S(1)} %bitcast.250, f32[1024,1024]{1,0:T(8,128)S(1)} %copy-done.1), kind=kOutput, calls=%fused_computation | convolution fusion | flops 1610743808 | bytes 5767168 | tf_op jit(solution)/shard_map/dot_general | solution.py:41
  321.8 13.9 %collective-permute-done.2 = f32[128,1024]{1,0:T(8,128)S(1)} collective-permute-done((f32[128,1024]{1,0:T(8,128)S(1)}, f32[128,1024]{1,0:T(8,128)S(1)}, u32[]{:S(2)}, u32[]{:S(2)}) %collective-permute-start.2) | collective-permute-done | bytes 524320 | tf_op jit(solution)/shard_map/ppermute | solution.py:16
  338.2 13.0 %all_to_all.215 = f32[128,8,128]{2,0,1:T(8,128)S(1)} all-to-all(f32[128,8,128]{2,0,1:T(8,128)S(1)} %bitcast.248), channel_id=1, replica_groups=mesh['tm_0'=4,'tm_1'=4,'space'=8] {'space'}, dimensions={1} | all-to-all | bytes 1048576 | tf_op jit(solution)/shard_map/all_to_all | solution.py:58
  353.7 4.5 %convolution_bitcast_fusion.1 = f32[16,8,8,128]{3,2,1,0:T(8,128)S(1)} fusion(f32[1024,128]{0,1:T(8,128)S(1)} %fusion, f32[1024,1024]{1,0:T(8,128)S(1)} %copy-done.1), kind=kOutput, calls=%fused_computation.2 | convolution fusion | flops 1610612736 | bytes 5242880 | tf_op jit(solution)/shard_map/dot_general | solution.py:41
  358.3 12.8 %all_to_all.216 = f32[8,128,128]{1,2,0:T(8,128)S(1)} all-to-all(f32[8,128,128]{1,2,0:T(8,128)S(1)} %bitcast.249), channel_id=1, replica_groups=mesh['tm_0'=4,'tm_1'=4,'space'=8] {'space'}, dimensions={0} | all-to-all | bytes 1048576 | tf_op jit(solution)/shard_map/all_to_all | solution.py:64
  371.0 5.4 %convolution_bitcast_fusion = f32[1,128,1024]{2,1,0:T(8,128)} fusion(f32[128,1024]{0,1:T(8,128)S(1)} %bitcast.241, f32[1024,1024]{1,0:T(8,128)S(1)} %copy-done.1), kind=kOutput, calls=%fused_computation.1 | convolution fusion | flops 1610612736 | bytes 5242880 | tf_op jit(solution)/shard_map/dot_general | solution.py:41
  (67 shorter events, 63.7 us)
Async XLA Ops:
  7.2 17.9 %collective-permute-start = (f32[128,1024]{1,0:T(8,128)}, f32[128,1024]{1,0:T(8,128)S(1)}, u32[]{:S(2)}, u32[]{:S(2)}) collective-permute-start(f32[128,1024]{1,0:T(8,128)} %bitcast.252), channel_id=1, source_target_pairs={{0,8},{8,16},{16,24},{24,32},{32,40},{40,48},{48,56},{56,64},{64,7... | collective-permute-start | bytes 1572872 | tf_op jit(solution)/shard_map/ppermute | solution.py:16
  10.7 25.3 %copy-start.7 = (f32[1024]{0:T(1024)S(1)}, f32[1024]{0:T(1024)}, u32[]{:S(2)}) copy-start(f32[1024]{0:T(1024)} %param.12) | copy-start | bytes 12292
  30.7 15.6 %all-to-all-start = ((f32[128,8,128]{2,0,1:T(8,128)}), f32[128,8,128]{2,0,1:T(8,128)S(1)}, u32[]{:S(2)}, u32[]{:S(2)}) async-start(f32[128,8,128]{2,0,1:T(8,128)} %bitcast.231), calls=%async_computation | async-start | bytes 1048576 | tf_op jit(solution)/shard_map/all_to_all | solution.py:58
  46.3 4.8 %copy-start = (f32[1024,1024]{1,0:T(8,128)S(1)}, f32[1024,1024]{1,0:T(8,128)}, u32[]{:S(2)}) copy-start(f32[1024,1024]{1,0:T(8,128)} %param.11) | copy-start | bytes 12582916
  55.5 18.0 %copy-start.5 = (f32[1,128,1024]{2,1,0:T(8,128)S(1)}, f32[1,128,1024]{2,1,0:T(8,128)}, u32[]{:S(2)}) copy-start(f32[1,128,1024]{2,1,0:T(8,128)} %param.10) | copy-start | bytes 1572868
  95.7 35.0 %copy-start.2 = (f32[1,128,1024]{2,1,0:T(8,128)S(1)}, f32[1,128,1024]{2,1,0:T(8,128)}, u32[]{:S(2)}) copy-start(f32[1,128,1024]{2,1,0:T(8,128)} %param.9) | copy-start | bytes 1572868
  95.7 35.0 %copy-start.3 = (f32[128,1024]{1,0:T(8,128)S(1)}, f32[128,1024]{1,0:T(8,128)}, u32[]{:S(2)}) copy-start(f32[128,1024]{1,0:T(8,128)} %param.7) | copy-start | bytes 1572868
  113.4 17.3 %collective-permute-start.1 = (f32[128,1024]{1,0:T(8,128)S(1)}, f32[128,1024]{1,0:T(8,128)S(1)}, u32[]{:S(2)}, u32[]{:S(2)}) collective-permute-start(f32[128,1024]{1,0:T(8,128)S(1)} %fusion.112), channel_id=1, source_target_pairs={{0,8},{8,16},{16,24},{24,32},{32,40},{40,48},{48,56},{56,64},{64,7... | collective-permute-start | bytes 1572872 | tf_op jit(solution)/shard_map/ppermute | solution.py:16
  173.6 14.1 %all-to-all-start.6 = ((f32[128,8,128]{2,0,1:T(8,128)}), f32[128,8,128]{2,0,1:T(8,128)S(1)}, u32[]{:S(2)}, u32[]{:S(2)}) async-start(f32[128,8,128]{2,0,1:T(8,128)} %bitcast.225), calls=%async_computation.6 | async-start | bytes 1048576 | tf_op jit(solution)/shard_map/all_to_all | solution.py:58
  187.7 13.7 %all-to-all-start.7 = ((f32[128,8,128]{2,0,1:T(8,128)}), f32[128,8,128]{2,0,1:T(8,128)S(1)}, u32[]{:S(2)}, u32[]{:S(2)}) async-start(f32[128,8,128]{2,0,1:T(8,128)} %bitcast.224), calls=%async_computation.7 | async-start | bytes 1048576 | tf_op jit(solution)/shard_map/all_to_all | solution.py:58
  191.2 43.6 %all-gather.6.cloned.1.call-start = ((), (), s32[]{:S(2)}) async-start(), calls=%async_computation.12 | async-start | bytes 2621440 | tf_op jit(solution)/shard_map/all_gather | solution.py:30
  198.0 9.2 %copy-start.9 = (u32[128]{0:T(128)S(1)}, u32[128]{0:T(128)}, u32[]{:S(2)}) copy-start(u32[128]{0:T(128)} %constant.43) | copy-start | bytes 1540
  201.5 43.7 %copy-start.8 = (u32[128]{0:T(128)S(1)}, u32[128]{0:T(128)}, u32[]{:S(2)}) copy-start(u32[128]{0:T(128)} %constant.48) | copy-start | bytes 1540
  207.1 65.4 %all-gather.4.cloned.1.call-start = ((), (), s32[]{:S(2)}) async-start(), calls=%async_computation.11 | async-start | bytes 2621440 | tf_op jit(solution)/shard_map/all_gather | solution.py:30
  256.5 23.9 %copy-start.4 = (f32[1024,128]{0,1:T(8,128)S(1)}, f32[1024,128]{0,1:T(8,128)}, u32[]{:S(2)}) copy-start(f32[1024,128]{0,1:T(8,128)} %fusion.2) | copy-start | bytes 1572868
  280.4 33.3 %copy-start.1 = (f32[1024,1024]{1,0:T(8,128)S(1)}, f32[1024,1024]{1,0:T(8,128)}, u32[]{:S(2)}) copy-start(f32[1024,1024]{1,0:T(8,128)} %param.11) | copy-start | bytes 12582916
  318.4 32.9 %copy-start.6 = (f32[128,1024]{1,0:T(8,128)}, f32[128,1024]{1,0:T(8,128)S(1)}, u32[]{:S(2)}) copy-start(f32[128,1024]{1,0:T(8,128)S(1)} %convolution_add_fusion) | copy-start | bytes 1572868
  318.4 17.3 %collective-permute-start.2 = (f32[128,1024]{1,0:T(8,128)S(1)}, f32[128,1024]{1,0:T(8,128)S(1)}, u32[]{:S(2)}, u32[]{:S(2)}) collective-permute-start(f32[128,1024]{1,0:T(8,128)S(1)} %convolution_add_fusion), channel_id=1, source_target_pairs={{0,8},{8,16},{16,24},{24,32},{32,40},{40,48},{48,56},{56,64},{64,7... | collective-permute-start | bytes 1572872 | tf_op jit(solution)/shard_map/ppermute | solution.py:16
Sparse Core Ops, SparseCore 0:
  207.2 27.6 all-gather.5
  242.7 29.7 all-gather.3
where the time goes:
time: 391 us; the launch traced here: 384 us
  blocking collectives  122 us (31%)
  matrix products  101 us (26%)
  waiting for transfers between devices  96.3 us (25%)
  starting transfers between devices  21.6 us (6%)
  between operations  18 us (5%)
  local copies, waits for them, and re-layouts  17.8 us (5%)
  other arithmetic  6.66 us (2%)
    dot_general x22, matrix products, product(): jnp.dot(left, right, preferred_element_type=jnp.float32, precision=exact_...  101 us
    all_to_all x5, blocking collectives, from_eigen(): lax.all_to_all(left, 'space', split_axis=0, concat_axis=1, tiled=True)  66.8 us
    ppermute x3, waiting for transfers between devices, passed_along(): return lax.ppermute(block, axis, route)  43.6 us
    all_to_all x3, blocking collectives, to_eigen(): lax.all_to_all(right, 'space', split_axis=1, concat_axis=0, tiled=True)  38.6 us
    all_gather x2, waiting for transfers between devices, prefix_by_axis(): pieces = jax.tree.map(lambda part: lax.all_gather(part, axis), subtotal)  34.1 us
    all_to_all x3, waiting for transfers between devices, to_eigen(): lax.all_to_all(right, 'space', split_axis=1, concat_axis=0, tiled=True)  18.5 us
    unnamed x2, blocking collectives  16.4 us
    all_to_all x3, starting transfers between devices, to_eigen(): lax.all_to_all(right, 'space', split_axis=1, concat_axis=0, tiled=True)  12.7 us
  transfers between devices with their start and end apart: 8, of which 8 were waited for; matrix products, arithmetic and copies ran while one was open for 4% of the time, Pallas kernels for 0%

commit v1 on v0

v1 whole, which is shorter than its diff:
```python
import jax
import jax.numpy as jnp
from jax import lax
from jax.experimental import pallas as pl
from jax.experimental.pallas import tpu as pltpu
from jax.sharding import PartitionSpec as P

MESH = pl.DeviceIdType.MESH
F32 = jnp.float32
BF16 = jnp.bfloat16
TM = 16
SPACE = 8
N = 1024
B = 128
H = B // 2
ORDER_OUT = (2, 1, 3, 0)
ORDER_IN = (0, 1, 3, 2)


def dot(a, b):
    return jnp.dot(a, b, preferred_element_type=F32)


def react(field):
    return field + 0.5 * jnp.tanh(field)


def split(x):
    hi = x.astype(BF16)
    return hi, (x - hi.astype(F32)).astype(BF16)


def kernel(
    init_h, guess_h, ff_h, fc_h, u_h, rates, carried_h,
    fs_o, cs_o,
    ubuf, uh, ul, th, tl, init, guess, ff, fc, carried,
    ga, ffn, nrf, nrfn, coef, coefp, csb,
    sw, w, sz, z_in, xs, yb, fd, rsum, yref, lacc, facc, srecv, ssend, crecv,
    u_sem, loc_sem, sh_send, sh_recv,
    w_send, w_recv, wb_send, wb_recv, z_send, z_recv,
    s_send, s_recv, c_send, c_recv, out_sem,
):
    tm = lax.axis_index("tm")
    me = lax.axis_index("space")
    zc = me // 2
    core = me % 2
    other = zc * 2 + (1 - core)
    nxt = lax.rem(tm + 1, TM)
    prv = lax.rem(tm + TM - 1, TM)

    def remote(src, dst, ss, rs, dev):
        return pltpu.make_async_remote_copy(
            src_ref=src, dst_ref=dst, send_sem=ss, recv_sem=rs, device_id=dev, device_id_type=MESH
        )

    u_copies = [
        pltpu.make_async_copy(u_h.at[pl.ds(i * 256, 256)], ubuf.at[pl.ds(i * 256, 256)], u_sem.at[i])
        for i in range(4)
    ]
    loads = [
        pltpu.make_async_copy(init_h, init, loc_sem.at[0]),
        pltpu.make_async_copy(guess_h, guess, loc_sem.at[1]),
        pltpu.make_async_copy(ff_h, ff, loc_sem.at[2]),
        pltpu.make_async_copy(fc_h, fc, loc_sem.at[3]),
        pltpu.make_async_copy(
            carried_h.at[pl.ds(pl.multiple_of(tm * 64, 64), 64), pl.ds(pl.multiple_of(me * B, B), B)],
            carried, loc_sem.at[4]),
    ]
    for c in u_copies:
        c.start()
    for c in loads:
        c.start()

    barrier = pltpu.get_barrier_semaphore()
    count = 0
    for d in range(1, SPACE):
        pl.semaphore_signal(barrier, inc=1, device_id=(tm, lax.rem(me + d, SPACE)), device_id_type=MESH)
        count += 1
    for d in range(1, TM):
        pl.semaphore_signal(barrier, inc=1, device_id=(lax.rem(tm + d, TM), me), device_id_type=MESH)
        count += 1
    for d in range(1, SPACE):
        for t in (nxt, prv):
            pl.semaphore_signal(barrier, inc=1, device_id=(t, lax.rem(me + d, SPACE)), device_id_type=MESH)
            count += 1
    pl.semaphore_wait(barrier, count)

    top, low = pl.ds(0, H), pl.ds(H, H)
    guess_shift = remote(guess_h.at[top], ga, sh_send.at[0], sh_recv.at[0], (nxt, me))
    force_shift = remote(ff_h.at[low], ffn.at[low], sh_send.at[1], sh_recv.at[1], (prv, me))
    guess_shift.start()
    force_shift.start()
    force_rest = remote(ff_h.at[top], ffn.at[top], sh_send.at[2], sh_recv.at[2], (prv, me))
    nrf_shift = remote(nrf, nrfn, sh_send.at[3], sh_recv.at[3], (prv, me))
    coef_shift = remote(coef, coefp, sh_send.at[4], sh_recv.at[4], (nxt, me))
    cs_shift = remote(csb, cs_o, sh_send.at[5], sh_recv.at[5], (prv, me))

    for i in range(4):
        u_copies[i].wait()

    def prep(i, carry):
        at = pl.ds(pl.multiple_of(i * B, B), B)
        hi, lo = split(ubuf[at, :])
        uh[at, :] = hi
        ul[at, :] = lo
        return carry

    lax.fori_loop(0, 8, prep, 0)

    own = rates[:, pl.ds(pl.multiple_of(me * B, B), B)]

    def prep_decay(i, carry):
        at = pl.ds(pl.multiple_of(i * B, B), B)
        down = jnp.broadcast_to(rates[:, at], (B, B)).T
        s = down + jnp.broadcast_to(own, (B, B))
        rsum[at, :] = s
        fd[at, :] = 1.0 / (1.0 + s)
        return carry

    lax.fori_loop(0, 8, prep_decay, 0)

    def prep_t(i, carry):
        at = pl.ds(pl.multiple_of(i * B, B), B)
        hi, lo = split(ubuf[at, :].T)
        th[:, at] = hi
        tl[:, at] = lo
        return carry

    def chip_of(q):
        return lax.rem(zc + q, 4)

    def right_send(first):
        xh = xs[pl.ds(0, B), :]
        for q in ORDER_OUT:
            zd = chip_of(q)
            cols = pl.ds(pl.multiple_of(zd * 256, 256), 256)
            a = dot(xs[...], uh[:, cols])
            p = a[:B] + a[B:] + dot(xh, ul[:, cols])
            sw[zd * 2] = p[:, :B]
            sw[zd * 2 + 1] = p[:, B:]
            for c in range(2):
                d = zd * 2 + c
                if first:
                    ca = remote(sw.at[d, top], w.at[me, top], w_send.at[d], w_recv.at[me], (tm, d))
                    cb = remote(sw.at[d, low], w.at[me, low], wb_send.at[d], wb_recv.at[me], (nxt, d))
                    cb.start()
                else:
                    ca = remote(sw.at[d], w.at[me], w_send.at[d], w_recv.at[me], (tm, d))
                if q:
                    ca.start()
                else:
                    pl.when(core != c)(ca.start)
        if first:
            w[me, top] = sw[me, top]
        else:
            w[me] = sw[me]

    def wait_w(s, first, full):
        if first:
            remote(sw.at[s, low], w.at[s, low], wb_send.at[s], wb_recv.at[s], (prv, s)).wait_recv()
        if full:
            if first:
                remote(sw.at[s, top], w.at[s, top], w_send.at[s], w_recv.at[s], (tm, s)).wait_recv()
            else:
                remote(sw.at[s], w.at[s], w_send.at[s], w_recv.at[s], (tm, s)).wait_recv()

    def wait_w_sent(d, first, full):
        if first:
            remote(sw.at[d, low], w.at[me, low], wb_send.at[d], wb_recv.at[me], (nxt, d)).wait_send()
        if full:
            if first:
                remote(sw.at[d, top], w.at[me, top], w_send.at[d], w_recv.at[me], (tm, d)).wait_send()
            else:
                remote(sw.at[d], w.at[me], w_send.at[d], w_recv.at[me], (tm, d)).wait_send()

    for c in loads:
        c.wait()
    guess_shift.wait_recv()
    x = react(jnp.where(tm == 0, init[top, :], ga[...])) + ff[top, :]
    hi, lo = split(x)
    xs[pl.ds(0, H), :] = hi
    xs[pl.ds(B, H), :] = lo
    force_shift.wait_recv()
    x = react(jnp.where(tm == TM - 1, init[low, :], guess[low, :])) + ffn[low, :]
    hi, lo = split(x)
    xs[pl.ds(H, H), :] = hi
    xs[pl.ds(B + H, H), :] = lo
    right_send(True)
    force_rest.start()
    lax.fori_loop(0, 8, prep_t, 0)

    def scan_groups():
        for d in range(1, TM):
            e = lax.rem(tm + d, TM)
            remote(yref.at[e], srecv.at[tm], s_send.at[e], s_recv.at[tm], (e, me)).start()
        srecv[tm] = yref[tm]
        cd = 1.0 / (1.0 + 2.0 * rsum[pl.ds(pl.multiple_of(tm * 64, 64), 64), :])
        corr = carried[...]
        for d in range(1, TM):
            e = lax.rem(tm + d, TM)
            remote(yref.at[e], srecv.at[e], s_send.at[e], s_recv.at[e], (e, me)).wait_recv()
        for g in range(TM):
            corr = cd * corr + srecv[(g + TM - 1) % TM]
            ssend[g] = corr
            dest = (g + 1) % TM
            pl.when(tm != dest)(
                remote(ssend.at[g], crecv.at[tm], c_send.at[g], c_recv.at[tm], (dest, me)).start
            )
        crecv[tm] = ssend[prv]
        for d in range(1, TM):
            e = lax.rem(tm + d, TM)
            remote(ssend.at[e], crecv.at[e], c_send.at[e], c_recv.at[e], (e, me)).wait_recv()
        for d in range(1, TM):
            e = lax.rem(tm + d, TM)
            remote(yref.at[e], srecv.at[e], s_send.at[e], s_recv.at[e], (e, me)).wait_send()
        for g in range(TM):
            dest = (g + 1) % TM
            pl.when(tm != dest)(
                remote(ssend.at[g], crecv.at[tm], c_send.at[g], c_recv.at[tm], (dest, me)).wait_send
            )
        coef_shift.wait()
        yref[...] = coefp[...].reshape(TM, 64, B) + crecv[...]

    def turn(k, carry):
        for n, q in enumerate(ORDER_IN):
            zs = chip_of(q)

            def waits(first):
                if q:
                    wait_w(zs * 2, first, True)
                    wait_w(zs * 2 + 1, first, True)
                else:
                    wait_w(other, first, True)
                    if first:
                        wait_w(me, True, False)

            pl.when(k == 0)(lambda: waits(True))
            pl.when(k > 0)(lambda: waits(False))
            cols = pl.ds(pl.multiple_of(zs * 256, 256), 256)
            hi, lo = split(w[pl.ds(zs * 2, 2)].reshape(256, B))
            a = dot(th[:, cols], jnp.concatenate([hi, lo], axis=1))
            v = a[:, :B] + a[:, B:] + dot(tl[:, cols], hi)
            if n == 0:
                lacc[...] = v
            else:
                lacc[...] += v

        def sent(first):
            for q in (1, 2, 3):
                wait_w_sent(chip_of(q) * 2, first, True)
                wait_w_sent(chip_of(q) * 2 + 1, first, True)
            wait_w_sent(other, first, True)
            if first:
                wait_w_sent(me, True, False)

        pl.when(k == 0)(lambda: sent(True))
        pl.when(k > 0)(lambda: sent(False))

        yref[...] = (fd[...] * lacc[...]).reshape(TM, 64, B)

        @pl.when(k == 1)
        def _():
            coef[...] = yref[...].reshape(N, B)
            coef_shift.start()

        pl.when(k == 3)(scan_groups)

        hi, lo = split(yref[...].reshape(N, B))
        yb[:, pl.ds(0, B)] = hi
        yb[:, pl.ds(B, B)] = lo

        for q in ORDER_OUT:
            zd = chip_of(q)
            rows = pl.ds(pl.multiple_of(zd * 256, 256), 256)
            a = dot(uh[rows, :], yb[...])
            v = a[:, :B] + a[:, B:] + dot(ul[rows, :], yb[:, pl.ds(0, B)])
            sz[zd * 2] = v[:B]
            sz[zd * 2 + 1] = v[B:]
            for c in range(2):
                d = zd * 2 + c
                cp = remote(sz.at[d], z_in.at[me], z_send.at[d], z_recv.at[me], (tm, d))
                if q:
                    cp.start()
                else:
                    pl.when(core != c)(cp.start)
        z_in[me] = sz[me]

        for n, q in enumerate(ORDER_IN):
            zs = chip_of(q)
            sources = (zs * 2, zs * 2 + 1) if q else (other,)
            for s in sources:
                remote(sz.at[s], z_in.at[s], z_send.at[s], z_recv.at[s], (tm, s)).wait_recv()
            rows = pl.ds(pl.multiple_of(zs * 256, 256), 256)
            hi, lo = split(jnp.concatenate([z_in[zs * 2], z_in[zs * 2 + 1]], axis=1))
            a = dot(jnp.concatenate([hi, lo], axis=0), th[rows, :])
            v = a[:B] + a[B:] + dot(hi, tl[rows, :])
            if n == 0:
                facc[...] = v
            else:
                facc[...] += v
        for q in (1, 2, 3):
            for c in range(2):
                d = chip_of(q) * 2 + c
                remote(sz.at[d], z_in.at[me], z_send.at[d], z_recv.at[me], (tm, d)).wait_send()
        remote(sz.at[other], z_in.at[me], z_send.at[other], z_recv.at[me], (tm, other)).wait_send()

        @pl.when(k == 3)
        def _():
            csb[...] = facc[...]
            cs_shift.start()

        @pl.when(k < 4)
        def _():
            restart = ((k == 1) & (tm == TM - 1)) | ((k == 3) & (tm == 0))
            facc[...] = react(jnp.where(restart, init[...], facc[...]))

            @pl.when(k == 0)
            def _():
                nrf[...] = facc[...]
                nrf_shift.start()
                facc[...] += fc[...]

            @pl.when(k == 1)
            def _():
                force_shift.wait_send()
                force_rest.wait()
                facc[...] += ffn[...]

            @pl.when(k == 2)
            def _():
                nrf_shift.wait()
                facc[...] -= nrfn[...]

            @pl.when(k == 3)
            def _():
                facc[...] += ff[...]

            hi, lo = split(facc[...])
            xs[pl.ds(0, B), :] = hi
            xs[pl.ds(B, B), :] = lo
            right_send(False)

        return carry

    lax.fori_loop(0, 5, turn, 0)
    out = pltpu.make_async_copy(facc, fs_o, out_sem)
    out.start()
    guess_shift.wait_send()
    cs_shift.wait()
    out.wait()


def on_device(initial_state, guess_coarse, force_fine, force_coarse, eigen_basis, eigen_rates, carried_correction):
    vm, dma = pltpu.VMEM, pltpu.SemaphoreType.DMA
    any_spec = pl.BlockSpec(memory_space=pl.ANY)
    field = vm((B, N), F32)
    half = vm((H, N), F32)
    column = vm((N, B), F32)
    blocks = vm((SPACE, B, B), F32)
    parts = vm((TM, 64, B), F32)
    basis = vm((N, N), BF16)
    fine, coarse = pl.pallas_call(
        kernel,
        out_shape=(jax.ShapeDtypeStruct((B, N), F32), jax.ShapeDtypeStruct((B, N), F32)),
        in_specs=[any_spec] * 5 + [pl.BlockSpec(memory_space=pltpu.VMEM), any_spec],
        out_specs=(any_spec, any_spec),
        scratch_shapes=[
            vm((N, N), F32), basis, basis, basis, basis,
            field, field, field, field, vm((64, B), F32),
            half, field, field, field, column, column, field,
            blocks, blocks, blocks, blocks,
            vm((2 * B, N), BF16), vm((N, 2 * B), BF16),
            column, column, parts, column, field, parts, parts, parts,
            dma((4,)), dma((5,)), dma((6,)), dma((6,)),
            dma((8,)), dma((8,)), dma((8,)), dma((8,)), dma((8,)), dma((8,)),
            dma((16,)), dma((16,)), dma((16,)), dma((16,)), dma,
        ],
        compiler_params=pltpu.CompilerParams(
            collective_id=0, has_side_effects=True, vmem_limit_bytes=48 * 1024 * 1024
        ),
        name="mgrit_cycle",
    )(
        initial_state, guess_coarse[0], force_fine[0], force_coarse[0],
        eigen_basis, eigen_rates[None, :], carried_correction,
    )
    return fine[None], coarse[None]


def solution(mesh):
    rows = P("tm", "space", None)
    return jax.shard_map(
        on_device,
        mesh=mesh,
        in_specs=(P("space", None), rows, rows, rows, P(), P(), P()),
        out_specs=(rows, rows),
        check_vma=False,
    )
```

time: 391 us -> 141 us (0.36)
  the two profiles are of different devices: /device:TPU:2 before, /device:TPU:1 now
where the time goes in v1:
time: 141 us
  Pallas kernels  134 us (95%)
  local copies, waits for them, and re-layouts  6.43 us (5%)
    pallas_call x1, Pallas kernels, on_device(): pl.pallas_call(kernel, out_shape=(jax.ShapeDtypeStruct((B, N), F32), jax....  134 us
    unnamed x12, local copies, waits for them, and re-layouts  6.43 us

profile of v1, /device:TPU:1, one launch (start us, length us, event | category | flops | bytes accessed | tf_op | source)
XLA Modules:
  0.0 140.9 jit_solution(9882076040227403156)
XLA Ops:
  0.6 0.0 copy-start
  0.6 1.0 copy-done
  1.7 0.0 copy-start.1
  1.7 1.0 copy-done.1
  2.7 0.0 copy-start.2
  2.7 1.0 copy-done.2
  3.8 0.0 copy-start.3
  3.8 1.0 copy-done.3
  4.8 0.0 copy-start.4
  4.8 0.7 copy-done.4
  5.5 133.8 %mgrit_cycle.1 = (f32[128,1024]{1,0:T(8,128)S(1)}, f32[128,1024]{1,0:T(8,128)S(1)}) custom-call(f32[128,1024]{1,0:T(8,128)S(1)} %copy-done, f32[128,1024]{1,0:T(8,128)S(1)} %bitcast.6, f32[128,1024]{1,0:T(8,128)S(1)} %bitcast.7, f32[128,1024]{1,0:T(8,128)S(1)} %bitcast.8, f32[1024,1024]{1,0:T(8,128)} %u_h.1, f32[1,1024]{1,0:T(1,128)S(1)} %bitcast.11, ...), custom_call_target="tpu_custom_call" | custom-call | tf_op jit(solution)/shard_map/mgrit_cycle/pallas_call | solution.py:362
  139.3 0.8 copy.11
  140.1 0.8 copy.12
Async XLA Ops:
  0.6 1.0 copy-start
  1.7 1.0 copy-start.1
  2.7 1.0 copy-start.2
  3.8 1.0 copy-start.3
  4.8 0.7 copy-start.4

commit v2 on v0

v2 whole, which is shorter than its diff:
```python
import jax
import jax.numpy as jnp
from jax import lax
from jax.experimental import pallas as pl
from jax.experimental.pallas import tpu as pltpu
from jax.sharding import PartitionSpec as P

MESH = pl.DeviceIdType.MESH
F32 = jnp.float32
BF16 = jnp.bfloat16
TM = 16
SPACE = 8
N = 1024
B = 128
H = B // 2
Q = H // 2
M = N // 2
E = M // TM
ORDER_OUT = (2, 1, 3, 0)
ORDER_IN = (0, 1, 3, 2)


def dot(a, b):
    return jnp.dot(a, b, preferred_element_type=F32)


def react(field):
    return field + 0.5 * jnp.tanh(field)


def split(x):
    hi = x.astype(BF16)
    return hi, (x - hi.astype(F32)).astype(BF16)


def kernel(
    init_h, guess_h, ff_h, fc_h, u_h, rates, carried_h,
    fs_o, cs_o,
    ubuf, uh, ul, th, tl, lu, lt, init, guess, ff, fc, carried,
    ga, ffn, nrf, nrfn, coef, coefp, csb,
    sw, w, sz, z_in, xs, yb, fd, rsum, yref, lacc, facc, srecv, ssend, crecv,
    u_sem, loc_sem, ga_send, ga_recv, fb_send, fb_recv, fa_send, fa_recv,
    nr_send, nr_recv, co_send, co_recv, cs_send, cs_recv,
    w_send, w_recv, wb_send, wb_recv, z_send, z_recv,
    s_send, s_recv, c_send, c_recv,
):
    tm = lax.axis_index("tm")
    me = lax.axis_index("space")
    zc = me // 2
    core = me % 2
    other = zc * 2 + (1 - core)
    nxt = lax.rem(tm + 1, TM)
    prv = lax.rem(tm + TM - 1, TM)

    def remote(src, dst, ss, rs, dev):
        return pltpu.make_async_remote_copy(
            src_ref=src, dst_ref=dst, send_sem=ss, recv_sem=rs, device_id=dev, device_id_type=MESH
        )

    def chip_of(q):
        return lax.rem(zc + q, 4)

    u_copies = [
        pltpu.make_async_copy(u_h.at[pl.ds(i * 256, 256)], ubuf.at[pl.ds(i * 256, 256)], u_sem.at[i])
        for i in range(4)
    ]
    own_cols = pl.ds(pl.multiple_of(me * B, B), B)
    loads = [
        pltpu.make_async_copy(init_h, init, loc_sem.at[0]),
        pltpu.make_async_copy(guess_h, guess, loc_sem.at[1]),
        pltpu.make_async_copy(ff_h, ff, loc_sem.at[2]),
        pltpu.make_async_copy(fc_h, fc, loc_sem.at[3]),
    ] + [
        pltpu.make_async_copy(
            carried_h.at[pl.ds(pl.multiple_of(m * M + tm * E, E), E), own_cols], carried.at[m], loc_sem.at[4 + m])
        for m in range(2)
    ]
    for c in u_copies + loads:
        c.start()

    barrier = pltpu.get_barrier_semaphore()
    count = 0
    for d in range(1, SPACE):
        for t in (tm, nxt, prv):
            pl.semaphore_signal(barrier, inc=1, device_id=(t, lax.rem(me + d, SPACE)), device_id_type=MESH)
            count += 1
    for d in range(1, TM):
        pl.semaphore_signal(barrier, inc=1, device_id=(lax.rem(tm + d, TM), me), device_id_type=MESH)
        count += 1

    for c in u_copies:
        c.wait()

    def prep_natural(i, carry):
        at = pl.ds(pl.multiple_of(i * B, B), B)
        hi, lo = split(ubuf[at, :])
        uh[at, :] = hi
        ul[at, :] = lo
        hi, lo = split(ubuf[at, :].T)
        th[:, at] = hi
        tl[:, at] = lo
        return carry

    def prep_halves(j, carry):
        row = (j % 4) * 256 + (j // 4) * H
        x = jnp.concatenate(
            [ubuf[pl.ds(pl.multiple_of(row, H), H), :], ubuf[pl.ds(pl.multiple_of(row + B, H), H), :]], axis=0
        )
        hi, lo = split(x)
        lu[j, pl.ds(0, B), :] = hi
        lu[j, pl.ds(B, B), :] = lo
        at = pl.ds(pl.multiple_of(j * B, B), B)
        hi, lo = split(x.T)
        for m in range(2):
            lt[m, pl.ds(0, M), at] = hi[m * M:(m + 1) * M]
            lt[m, pl.ds(M, M), at] = lo[m * M:(m + 1) * M]
        return carry

    lax.fori_loop(0, 8, prep_natural, 0)
    own = rates[:, own_cols]

    def prep_decay(i, carry):
        at = pl.ds(pl.multiple_of(i * B, B), B)
        down = jnp.broadcast_to(rates[:, at], (B, B)).T
        s = down + jnp.broadcast_to(own, (B, B))
        rsum[at, :] = s
        fd[at, :] = 1.0 / (1.0 + s)
        return carry

    lax.fori_loop(0, 8, prep_decay, 0)
    for c in loads:
        c.wait()

    pl.semaphore_wait(barrier, count)

    def part_a(h):
        return pl.ds(h * H, Q)

    def part_b(h):
        return pl.ds(h * H + Q, Q)

    def rows_of(h):
        return pl.ds(h * H, H)

    guess_shift = [remote(guess_h.at[part_a(h)], ga.at[h], ga_send.at[h], ga_recv.at[h], (nxt, me)) for h in range(2)]
    force_b = [remote(ff_h.at[part_b(h)], ffn.at[part_b(h)], fb_send.at[h], fb_recv.at[h], (prv, me)) for h in range(2)]
    force_a = [remote(ff_h.at[part_a(h)], ffn.at[part_a(h)], fa_send.at[h], fa_recv.at[h], (prv, me)) for h in range(2)]
    nrf_shift = [remote(nrf.at[rows_of(h)], nrfn.at[rows_of(h)], nr_send.at[h], nr_recv.at[h], (prv, me)) for h in range(2)]
    coef_shift = remote(coef, coefp, co_send, co_recv, (nxt, me))
    cs_shift = [remote(csb.at[rows_of(h)], cs_o.at[rows_of(h)], cs_send.at[h], cs_recv.at[h], (prv, me)) for h in range(2)]
    for h in range(2):
        guess_shift[h].start()
        force_b[h].start()

    keep, give = pl.ds(0, Q), pl.ds(Q, Q)

    def w_copies(h, s, d, first):
        if not first:
            return (remote(sw.at[h, d], w.at[h, s], w_send.at[h, d], w_recv.at[h, s], (tm, d)),)
        return (
            remote(sw.at[h, d, keep], w.at[h, s, keep], w_send.at[h, d], w_recv.at[h, s], (tm, d)),
            remote(sw.at[h, d, give], w.at[h, s, give], wb_send.at[h, d], wb_recv.at[h, s], (nxt, d)),
        )

    def z_copy(h, s, d):
        return remote(sz.at[h, d], z_in.at[h, s], z_send.at[h, d], z_recv.at[h, s], (tm, d))

    def right_send(h, first):
        for q in ORDER_OUT:
            zd = chip_of(q)
            cols = pl.ds(pl.multiple_of(zd * 256, 256), 256)
            a = dot(xs[h], uh[:, cols])
            p = a[:H] + a[H:] + dot(xs[h, pl.ds(0, H), :], ul[:, cols])
            for c in range(2):
                d = zd * 2 + c
                sw[h, d] = p[:, c * B:(c + 1) * B]
                copies = w_copies(h, me, d, first)
                if q:
                    copies[0].start()
                else:
                    pl.when(core != c)(copies[0].start)
                if first:
                    copies[1].start()
        if first:
            w[h, me, keep] = sw[h, me, keep]
        else:
            w[h, me] = sw[h, me]

    def wait_w(h, q, first):
        if q:
            zs = chip_of(q)
            for s in (zs * 2, zs * 2 + 1):
                for c in w_copies(h, s, s, first):
                    c.wait_recv()
        else:
            for c in w_copies(h, other, other, first):
                c.wait_recv()
            if first:
                w_copies(h, me, me, True)[1].wait_recv()

    def wait_w_sent(first):
        for h in range(2):
            for q in (1, 2, 3):
                for i in range(2):
                    for c in w_copies(h, me, chip_of(q) * 2 + i, first):
                        c.wait_send()
            for c in w_copies(h, me, other, first):
                c.wait_send()
            if first:
                w_copies(h, me, me, True)[1].wait_send()

    def put_xs(h, x):
        hi, lo = split(x)
        xs[h, pl.ds(0, H), :] = hi
        xs[h, pl.ds(H, H), :] = lo

    for h in range(2):
        guess_shift[h].wait_recv()
        xa = react(jnp.where(tm == 0, init[part_a(h), :], ga[h])) + ff[part_a(h), :]
        force_b[h].wait_recv()
        xb = react(jnp.where(tm == TM - 1, init[part_b(h), :], guess[part_b(h), :])) + ffn[part_b(h), :]
        put_xs(h, jnp.concatenate([xa, xb], axis=0))
        right_send(h, True)
    for h in range(2):
        force_a[h].start()
    lax.fori_loop(0, 8, prep_halves, 0)

    def parts(m, e):
        return pl.ds(m * M + e * E, E)

    def s_copy(m, e, slot):
        at = pl.ds(pl.multiple_of(m * M + e * E, E), E)
        return remote(yref.at[at], srecv.at[m, slot], s_send.at[m, e], s_recv.at[m, slot], (e, me))

    def c_copy(m, g, dev, slot):
        return remote(ssend.at[m, g], crecv.at[m, slot], c_send.at[m, g], c_recv.at[m, slot], (dev, me))

    def send_residual(m):
        for d in range(1, TM):
            s_copy(m, lax.rem(tm + d, TM), tm).start()
        srecv[m, tm] = yref[pl.ds(pl.multiple_of(m * M + tm * E, E), E), :]

    def scan_groups():
        for m in range(2):
            cd = 1.0 / (1.0 + 2.0 * rsum[pl.ds(pl.multiple_of(m * M + tm * E, E), E), :])
            corr = carried[m]
            for d in range(1, TM):
                e = lax.rem(tm + d, TM)
                s_copy(m, e, e).wait_recv()
            for g in range(TM):
                corr = cd * corr + srecv[m, (g + TM - 1) % TM]
                ssend[m, g] = corr
                dest = (g + 1) % TM
                pl.when(tm != dest)(c_copy(m, g, dest, tm).start)
            crecv[m, tm] = ssend[m, prv]
        coef_shift.wait()
        for m in range(2):
            for d in range(1, TM):
                e = lax.rem(tm + d, TM)
                s_copy(m, e, tm).wait_send()
            for d in range(1, TM):
                e = lax.rem(tm + d, TM)
                c_copy(m, e, e, e).wait_recv()
            at = pl.ds(m * M, M)
            yref[at, :] = coefp[at, :] + crecv[m].reshape(M, B)
        for m in range(2):
            for g in range(TM):
                dest = (g + 1) % TM
                pl.when(tm != dest)(c_copy(m, g, dest, tm).wait_send)

    def turn(k, carry):
        def wide(x):
            hi, lo = split(x)
            return jnp.concatenate([hi, lo], axis=1)

        def left_part(m, cols, ww):
            a = dot(lt[m, :, cols], ww)
            return a[:M, :B] + a[:M, B:] + a[M:, :B]

        def waits(h, qs):
            def go(first):
                for q in qs:
                    wait_w(h, q, first)
            pl.when(k == 0)(lambda: go(True))
            pl.when(k > 0)(lambda: go(False))

        waits(0, ORDER_IN)
        ww = wide(w[0].reshape(M, B))
        for m in range(2):
            lacc[m] = left_part(m, pl.ds(0, M), ww)
        for n, q in enumerate(ORDER_IN):
            zs = chip_of(q)
            waits(1, (q,))
            cols = pl.ds(pl.multiple_of(M + zs * B, B), B)
            ww = wide(w[1, pl.ds(zs * 2, 2)].reshape(B, B))
            for m in range(2):
                v = lacc[m] + left_part(m, cols, ww)
                if n < 3:
                    lacc[m] = v
                else:
                    at = pl.ds(m * M, M)
                    yref[at, :] = fd[at, :] * v
                    pl.when(k == 3)(lambda m=m: send_residual(m))
        pl.when(k == 0)(lambda: wait_w_sent(True))
        pl.when(k > 0)(lambda: wait_w_sent(False))

        @pl.when(k == 1)
        def _():
            coef[...] = yref[...]
            coef_shift.start()

        pl.when(k == 3)(scan_groups)

        yb[...] = wide(yref[...])

        for h in range(2):
            for q in ORDER_OUT:
                zd = chip_of(q)
                a = dot(lu[h * 4 + zd], yb[...])
                v = a[:B, :B] + a[:B, B:] + a[B:, :B]
                for c in range(2):
                    d = zd * 2 + c
                    sz[h, d] = v[c * H:(c + 1) * H]
                    cp = z_copy(h, me, d)
                    if q:
                        cp.start()
                    else:
                        pl.when(core != c)(cp.start)
            z_in[h, me] = sz[h, me]

        for h in range(2):
            for q in ORDER_IN:
                zs = chip_of(q)
                for s in (zs * 2, zs * 2 + 1) if q else (other,):
                    z_copy(h, s, s).wait_recv()
            rows = rows_of(h)
            hi, lo = split(jnp.concatenate([z_in[h, s] for s in range(SPACE)], axis=1))
            a = dot(jnp.concatenate([hi, lo], axis=0), th[...])
            facc[rows, :] = a[:H] + a[H:] + dot(hi, tl[...])

            @pl.when(k == 3)
            def _():
                csb[rows, :] = facc[rows, :]
                cs_shift[h].start()

            @pl.when(k < 4)
            def _():
                restart = ((k == 1) & (tm == TM - 1)) | ((k == 3) & (tm == 0))
                facc[rows, :] = react(jnp.where(restart, init[rows, :], facc[rows, :]))

                @pl.when(k == 0)
                def _():
                    nrf[rows, :] = facc[rows, :]
                    nrf_shift[h].start()
                    facc[rows, :] += fc[rows, :]

                @pl.when(k == 1)
                def _():
                    force_b[h].wait_send()
                    force_a[h].wait()
                    facc[rows, :] += ffn[rows, :]

                @pl.when(k == 2)
                def _():
                    nrf_shift[h].wait()
                    facc[rows, :] -= nrfn[rows, :]

                @pl.when(k == 3)
                def _():
                    facc[rows, :] += ff[rows, :]

                put_xs(h, facc[rows, :])
                right_send(h, False)

        for h in range(2):
            for q in (1, 2, 3):
                for c in range(2):
                    z_copy(h, me, chip_of(q) * 2 + c).wait_send()
            z_copy(h, me, other).wait_send()
        return carry

    lax.fori_loop(0, 5, turn, 0)
    fs_o[...] = facc[...]
    for h in range(2):
        guess_shift[h].wait_send()
        cs_shift[h].wait()


def on_device(initial_state, guess_coarse, force_fine, force_coarse, eigen_basis, eigen_rates, carried_correction):
    vm, dma = pltpu.VMEM, pltpu.SemaphoreType.DMA
    hbm = pl.BlockSpec(memory_space=pl.ANY)
    vmem = pl.BlockSpec(memory_space=pltpu.VMEM)
    field = vm((B, N), F32)
    column = vm((N, B), F32)
    blocks = vm((2, SPACE, H, B), F32)
    shares = vm((2, TM, E, B), F32)
    basis = vm((N, N), BF16)
    two, eight, sixteen = dma((2,)), dma((2, SPACE)), dma((2, TM))
    fine, coarse = pl.pallas_call(
        kernel,
        out_shape=(jax.ShapeDtypeStruct((B, N), F32), jax.ShapeDtypeStruct((B, N), F32)),
        in_specs=[hbm] * 5 + [vmem, hbm],
        out_specs=(vmem, vmem),
        scratch_shapes=[
            vm((N, N), F32), basis, basis, basis, basis,
            vm((8, 2 * B, N), BF16), vm((2, N, N), BF16),
            field, field, field, field, vm((2, E, B), F32),
            vm((2, Q, N), F32), field, field, field, column, column, field,
            blocks, blocks, blocks, blocks,
            vm((2, B, N), BF16), vm((N, 2 * B), BF16),
            column, column, column, vm((2, M, B), F32), field, shares, shares, shares,
            dma((4,)), dma((6,)), two, two, two, two, two, two,
            two, two, dma, dma, two, two,
            eight, eight, eight, eight, eight, eight,
            sixteen, sixteen, sixteen, sixteen,
        ],
        compiler_params=pltpu.CompilerParams(
            collective_id=0, has_side_effects=True, vmem_limit_bytes=48 * 1024 * 1024
        ),
        name="mgrit_cycle",
    )(
        initial_state, guess_coarse[0], force_fine[0], force_coarse[0],
        eigen_basis, eigen_rates[None, :], carried_correction,
    )
    return fine[None], coarse[None]


def solution(mesh):
    rows = P("tm", "space", None)
    return jax.shard_map(
        on_device,
        mesh=mesh,
        in_specs=(P("space", None), rows, rows, rows, P(), P(), P()),
        out_specs=(rows, rows),
        check_vma=False,
    )
```

time: 391 us -> 130 us (0.33)
  the two profiles are of different devices: /device:TPU:2 before, /device:TPU:1 now
where the time goes in v2:
time: 130 us; the launch traced here: 129 us
  Pallas kernels  122 us (94%)
  local copies, waits for them, and re-layouts  6.43 us (5%)
    pallas_call x1, Pallas kernels, on_device(): pl.pallas_call(kernel, out_shape=(jax.ShapeDtypeStruct((B, N), F32), jax....  122 us
    unnamed x12, local copies, waits for them, and re-layouts  6.43 us

profile of v2, /device:TPU:1, one launch (start us, length us, event | category | flops | bytes accessed | tf_op | source)
XLA Modules:
  0.0 129.3 jit_solution(16633150552345936661)
XLA Ops:
  0.6 0.0 copy-start
  0.6 1.0 copy-done
  1.7 0.0 copy-start.1
  1.7 1.0 copy-done.1
  2.7 0.0 copy-start.2
  2.7 1.0 copy-done.2
  3.8 0.0 copy-start.3
  3.8 1.0 copy-done.3
  4.8 0.0 copy-start.4
  4.8 0.7 copy-done.4
  5.5 122.2 %mgrit_cycle.1 = (f32[128,1024]{1,0:T(8,128)S(1)}, f32[128,1024]{1,0:T(8,128)S(1)}) custom-call(f32[128,1024]{1,0:T(8,128)S(1)} %copy-done, f32[128,1024]{1,0:T(8,128)S(1)} %bitcast.6, f32[128,1024]{1,0:T(8,128)S(1)} %bitcast.7, f32[128,1024]{1,0:T(8,128)S(1)} %bitcast.8, f32[1024,1024]{1,0:T(8,128)} %u_h.1, f32[1,1024]{1,0:T(1,128)S(1)} %bitcast.11, ...), custom_call_target="tpu_custom_call" | custom-call | tf_op jit(solution)/shard_map/mgrit_cycle/pallas_call | solution.py:399
  127.7 0.8 copy.11
  128.5 0.8 copy.12
Async XLA Ops:
  0.6 1.0 copy-start
  1.7 1.0 copy-start.1
  2.7 1.0 copy-start.2
  3.8 1.0 copy-start.3
  4.8 0.7 copy-start.4

commit v3 on v2

--- a/solution.py
+++ b/solution.py
@@ -16,8 +16,9 @@
 Q = H // 2
 M = N // 2
 E = M // TM
-ORDER_OUT = (2, 1, 3, 0)
-ORDER_IN = (0, 1, 3, 2)
+FAR_FIRST = sorted(
+    ((x, y) for x in range(4) for y in range(4) if x or y), key=lambda t: -min(t[0], 4 - t[0]) - min(t[1], 4 - t[1])
+)
 
 
 def dot(a, b):
@@ -60,6 +61,15 @@
     def chip_of(q):
         return lax.rem(zc + q, 4)
 
+    def partner(chip):
+        return chip + 1 - 2 * (chip % 2)
+
+    far, near = chip_of(2), partner(zc)
+    pairs = ((far // 2, (far, partner(far))), (zc // 2, (near, zc)))
+
+    def group_at(dx, dy):
+        return lax.rem(tm // 4 + dx, 4) * 4 + lax.rem(tm % 4 + dy, 4)
+
     u_copies = [
         pltpu.make_async_copy(u_h.at[pl.ds(i * 256, 256)], ubuf.at[pl.ds(i * 256, 256)], u_sem.at[i])
         for i in range(4)
@@ -88,6 +98,29 @@
         pl.semaphore_signal(barrier, inc=1, device_id=(lax.rem(tm + d, TM), me), device_id_type=MESH)
         count += 1
 
+    for c in loads:
+        c.wait()
+    pl.semaphore_wait(barrier, count)
+
+    def part_a(h):
+        return pl.ds(h * H, Q)
+
+    def part_b(h):
+        return pl.ds(h * H + Q, Q)
+
+    def rows_of(h):
+        return pl.ds(h * H, H)
+
+    guess_shift = [remote(guess.at[part_a(h)], ga.at[h], ga_send.at[h], ga_recv.at[h], (nxt, me)) for h in range(2)]
+    force_b = [remote(ff.at[part_b(h)], ffn.at[part_b(h)], fb_send.at[h], fb_recv.at[h], (prv, me)) for h in range(2)]
+    force_a = [remote(ff.at[part_a(h)], ffn.at[part_a(h)], fa_send.at[h], fa_recv.at[h], (prv, me)) for h in range(2)]
+    nrf_shift = [remote(nrf.at[rows_of(h)], nrfn.at[rows_of(h)], nr_send.at[h], nr_recv.at[h], (prv, me)) for h in range(2)]
+    coef_shift = remote(coef, coefp, co_send, co_recv, (nxt, me))
+    cs_shift = [remote(csb.at[rows_of(h)], cs_o.at[rows_of(h)], cs_send.at[h], cs_recv.at[h], (prv, me)) for h in range(2)]
+    for h in range(2):
+        guess_shift[h].start()
+        force_b[h].start()
+
     for c in u_copies:
         c.wait()
 
@@ -107,8 +140,9 @@
             [ubuf[pl.ds(pl.multiple_of(row, H), H), :], ubuf[pl.ds(pl.multiple_of(row + B, H), H), :]], axis=0
         )
         hi, lo = split(x)
-        lu[j, pl.ds(0, B), :] = hi
-        lu[j, pl.ds(B, B), :] = lo
+        at = pl.multiple_of(j % 2 * B, B)
+        lu[j // 2, pl.ds(at, B), :] = hi
+        lu[j // 2, pl.ds(2 * B + at, B), :] = lo
         at = pl.ds(pl.multiple_of(j * B, B), B)
         hi, lo = split(x.T)
         for m in range(2):
@@ -128,29 +162,6 @@
         return carry
 
     lax.fori_loop(0, 8, prep_decay, 0)
-    for c in loads:
-        c.wait()
-
-    pl.semaphore_wait(barrier, count)
-
-    def part_a(h):
-        return pl.ds(h * H, Q)
-
-    def part_b(h):
-        return pl.ds(h * H + Q, Q)
-
-    def rows_of(h):
-        return pl.ds(h * H, H)
-
-    guess_shift = [remote(guess_h.at[part_a(h)], ga.at[h], ga_send.at[h], ga_recv.at[h], (nxt, me)) for h in range(2)]
-    force_b = [remote(ff_h.at[part_b(h)], ffn.at[part_b(h)], fb_send.at[h], fb_recv.at[h], (prv, me)) for h in range(2)]
-    force_a = [remote(ff_h.at[part_a(h)], ffn.at[part_a(h)], fa_send.at[h], fa_recv.at[h], (prv, me)) for h in range(2)]
-    nrf_shift = [remote(nrf.at[rows_of(h)], nrfn.at[rows_of(h)], nr_send.at[h], nr_recv.at[h], (prv, me)) for h in range(2)]
-    coef_shift = remote(coef, coefp, co_send, co_recv, (nxt, me))
-    cs_shift = [remote(csb.at[rows_of(h)], cs_o.at[rows_of(h)], cs_send.at[h], cs_recv.at[h], (prv, me)) for h in range(2)]
-    for h in range(2):
-        guess_shift[h].start()
-        force_b[h].start()
 
     keep, give = pl.ds(0, Q), pl.ds(Q, Q)
 
@@ -166,21 +177,21 @@
         return remote(sz.at[h, d], z_in.at[h, s], z_send.at[h, d], z_recv.at[h, s], (tm, d))
 
     def right_send(h, first):
-        for q in ORDER_OUT:
-            zd = chip_of(q)
-            cols = pl.ds(pl.multiple_of(zd * 256, 256), 256)
+        for pr, chips in pairs:
+            cols = pl.ds(pl.multiple_of(pr * M, M), M)
             a = dot(xs[h], uh[:, cols])
             p = a[:H] + a[H:] + dot(xs[h, pl.ds(0, H), :], ul[:, cols])
-            for c in range(2):
-                d = zd * 2 + c
-                sw[h, d] = p[:, c * B:(c + 1) * B]
-                copies = w_copies(h, me, d, first)
-                if q:
-                    copies[0].start()
-                else:
-                    pl.when(core != c)(copies[0].start)
-                if first:
-                    copies[1].start()
+            for i in range(4):
+                sw[h, pr * 4 + i] = p[:, i * B:(i + 1) * B]
+            for zd in chips:
+                for c in range(2):
+                    copies = w_copies(h, me, zd * 2 + c, first)
+                    if zd is zc:
+                        pl.when(core != c)(copies[0].start)
+                    else:
+                        copies[0].start()
+                    if first:
+                        copies[1].start()
         if first:
             w[h, me, keep] = sw[h, me, keep]
         else:
@@ -236,8 +247,8 @@
         return remote(ssend.at[m, g], crecv.at[m, slot], c_send.at[m, g], c_recv.at[m, slot], (dev, me))
 
     def send_residual(m):
-        for d in range(1, TM):
-            s_copy(m, lax.rem(tm + d, TM), tm).start()
+        for dx, dy in FAR_FIRST:
+            s_copy(m, group_at(dx, dy), tm).start()
         srecv[m, tm] = yref[pl.ds(pl.multiple_of(m * M + tm * E, E), E), :]
 
     def scan_groups():
@@ -249,10 +260,11 @@
                 s_copy(m, e, e).wait_recv()
             for g in range(TM):
                 corr = cd * corr + srecv[m, (g + TM - 1) % TM]
-                ssend[m, g] = corr
-                dest = (g + 1) % TM
-                pl.when(tm != dest)(c_copy(m, g, dest, tm).start)
-            crecv[m, tm] = ssend[m, prv]
+                ssend[m, (g + 1) % TM] = corr
+            for dx, dy in FAR_FIRST:
+                dest = group_at(dx, dy)
+                c_copy(m, dest, dest, tm).start()
+            crecv[m, tm] = ssend[m, tm]
         coef_shift.wait()
         for m in range(2):
             for d in range(1, TM):
@@ -264,9 +276,9 @@
             at = pl.ds(m * M, M)
             yref[at, :] = coefp[at, :] + crecv[m].reshape(M, B)
         for m in range(2):
-            for g in range(TM):
-                dest = (g + 1) % TM
-                pl.when(tm != dest)(c_copy(m, g, dest, tm).wait_send)
+            for d in range(1, TM):
+                e = lax.rem(tm + d, TM)
+                c_copy(m, e, e, tm).wait_send()
 
     def turn(k, carry):
         def wide(x):
@@ -284,23 +296,16 @@
             pl.when(k == 0)(lambda: go(True))
             pl.when(k > 0)(lambda: go(False))
 
-        waits(0, ORDER_IN)
+        waits(0, range(4))
         ww = wide(w[0].reshape(M, B))
         for m in range(2):
             lacc[m] = left_part(m, pl.ds(0, M), ww)
-        for n, q in enumerate(ORDER_IN):
-            zs = chip_of(q)
-            waits(1, (q,))
-            cols = pl.ds(pl.multiple_of(M + zs * B, B), B)
-            ww = wide(w[1, pl.ds(zs * 2, 2)].reshape(B, B))
-            for m in range(2):
-                v = lacc[m] + left_part(m, cols, ww)
-                if n < 3:
-                    lacc[m] = v
-                else:
-                    at = pl.ds(m * M, M)
-                    yref[at, :] = fd[at, :] * v
-                    pl.when(k == 3)(lambda m=m: send_residual(m))
+        waits(1, range(4))
+        ww = wide(w[1].reshape(M, B))
+        for m in range(2):
+            at = pl.ds(m * M, M)
+            yref[at, :] = fd[at, :] * (lacc[m] + left_part(m, pl.ds(M, M), ww))
+            pl.when(k == 3)(lambda m=m: send_residual(m))
         pl.when(k == 0)(lambda: wait_w_sent(True))
         pl.when(k > 0)(lambda: wait_w_sent(False))
 
@@ -314,22 +319,22 @@
         yb[...] = wide(yref[...])
 
         for h in range(2):
-            for q in ORDER_OUT:
-                zd = chip_of(q)
-                a = dot(lu[h * 4 + zd], yb[...])
-                v = a[:B, :B] + a[:B, B:] + a[B:, :B]
-                for c in range(2):
-                    d = zd * 2 + c
-                    sz[h, d] = v[c * H:(c + 1) * H]
-                    cp = z_copy(h, me, d)
-                    if q:
-                        cp.start()
-                    else:
-                        pl.when(core != c)(cp.start)
+            for pr, chips in pairs:
+                a = dot(lu[h * 2 + pr], yb[...])
+                v = a[:2 * B, :B] + a[:2 * B, B:] + a[2 * B:, :B]
+                for i in range(4):
+                    sz[h, pr * 4 + i] = v[i * H:(i + 1) * H]
+                for zd in chips:
+                    for c in range(2):
+                        cp = z_copy(h, me, zd * 2 + c)
+                        if zd is zc:
+                            pl.when(core != c)(cp.start)
+                        else:
+                            cp.start()
             z_in[h, me] = sz[h, me]
 
         for h in range(2):
-            for q in ORDER_IN:
+            for q in range(4):
                 zs = chip_of(q)
                 for s in (zs * 2, zs * 2 + 1) if q else (other,):
                     z_copy(h, s, s).wait_recv()
@@ -403,7 +408,7 @@
         out_specs=(vmem, vmem),
         scratch_shapes=[
             vm((N, N), F32), basis, basis, basis, basis,
-            vm((8, 2 * B, N), BF16), vm((2, N, N), BF16),
+            vm((4, 4 * B, N), BF16), vm((2, N, N), BF16),
             field, field, field, field, vm((2, E, B), F32),
             vm((2, Q, N), F32), field, field, field, column, column, field,
             blocks, blocks, blocks, blocks,
@@ -415,7 +420,7 @@
             sixteen, sixteen, sixteen, sixteen,
         ],
         compiler_params=pltpu.CompilerParams(
-            collective_id=0, has_side_effects=True, vmem_limit_bytes=48 * 1024 * 1024
+            collective_id=0, has_side_effects=True, vmem_limit_bytes=56000000
         ),
         name="mgrit_cycle",
     )(

time: 130 us -> 124 us (0.954)
  local copies, waits for them, and re-layouts: 6.43 us -> 3.36 us
  Pallas kernels: 122 us -> 120 us
    unnamed x12 -> x4, local copies, waits for them, and re-layouts: 6.43 us -> 3.36 us
    pallas_call x1, Pallas kernels: 122 us -> 120 us  [on_device(): pl.pallas_call(kernel, out_shape=(jax.ShapeDtypeStruct((B, N), F32), jax....]
where the time goes in v3:
time: 124 us
  Pallas kernels  120 us (97%)
  local copies, waits for them, and re-layouts  3.36 us (3%)
    pallas_call x1, Pallas kernels, on_device(): pl.pallas_call(kernel, out_shape=(jax.ShapeDtypeStruct((B, N), F32), jax....  120 us
    unnamed x4, local copies, waits for them, and re-layouts  3.36 us

profile of v3, /device:TPU:1, one launch (start us, length us, event | category | flops | bytes accessed | tf_op | source)
XLA Modules:
  0.0 124.2 jit_solution(11410175258392268896)
XLA Ops:
  0.6 0.0 copy-start
  0.6 0.7 copy-done
  1.3 120.1 %mgrit_cycle.1 = (f32[128,1024]{1,0:T(8,128)S(1)}, f32[128,1024]{1,0:T(8,128)}) custom-call(f32[128,1024]{1,0:T(8,128)} %init_h.1, f32[128,1024]{1,0:T(8,128)} %bitcast.8, f32[128,1024]{1,0:T(8,128)} %bitcast.9, f32[128,1024]{1,0:T(8,128)} %bitcast.10, f32[1024,1024]{1,0:T(8,128)} %u_h.1, f32[1,1024]{1,0:T(1,128)S(1)} %bitcast.7, f32[1024,1024]{1,0:T(8,128)} %carried_h.1), custom_call_target="tpu_custom_call" | custom-call | tf_op jit(solution)/shard_map/mgrit_cycle/pallas_call | solution.py:404
  121.5 0.8 copy.11
  122.3 1.9 %copy.12 = f32[1,128,1024]{2,1,0:T(8,128)} copy(f32[1,128,1024]{2,1,0:T(8,128)} %bitcast.11) | data formatting | bytes 1048576
Async XLA Ops:
  0.6 0.7 copy-start

commit v4 on v3

--- a/solution.py
+++ b/solution.py
@@ -15,7 +15,7 @@
 H = B // 2
 Q = H // 2
 M = N // 2
-E = M // TM
+E = B // TM
 FAR_FIRST = sorted(
     ((x, y) for x in range(4) for y in range(4) if x or y), key=lambda t: -min(t[0], 4 - t[0]) - min(t[1], 4 - t[1])
 )
@@ -37,7 +37,7 @@
 def kernel(
     init_h, guess_h, ff_h, fc_h, u_h, rates, carried_h,
     fs_o, cs_o,
-    ubuf, uh, ul, th, tl, lu, lt, init, guess, ff, fc, carried,
+    ubuf, uh, ul, th, tl, uph, upl, tph, tpl, init, guess, ff, fc, cbuf, carried,
     ga, ffn, nrf, nrfn, coef, coefp, csb,
     sw, w, sz, z_in, xs, yb, fd, rsum, yref, lacc, facc, srecv, ssend, crecv,
     u_sem, loc_sem, ga_send, ga_recv, fb_send, fb_recv, fa_send, fa_recv,
@@ -80,10 +80,7 @@
         pltpu.make_async_copy(guess_h, guess, loc_sem.at[1]),
         pltpu.make_async_copy(ff_h, ff, loc_sem.at[2]),
         pltpu.make_async_copy(fc_h, fc, loc_sem.at[3]),
-    ] + [
-        pltpu.make_async_copy(
-            carried_h.at[pl.ds(pl.multiple_of(m * M + tm * E, E), E), own_cols], carried.at[m], loc_sem.at[4 + m])
-        for m in range(2)
+        pltpu.make_async_copy(carried_h.at[:, own_cols], cbuf, loc_sem.at[4]),
     ]
     for c in u_copies + loads:
         c.start()
@@ -136,29 +133,29 @@
 
     def prep_halves(j, carry):
         row = (j % 4) * 256 + (j // 4) * H
-        x = jnp.concatenate(
-            [ubuf[pl.ds(pl.multiple_of(row, H), H), :], ubuf[pl.ds(pl.multiple_of(row + B, H), H), :]], axis=0
-        )
+        first, second = pl.ds(pl.multiple_of(row, H), H), pl.ds(pl.multiple_of(row + B, H), H)
+        at = pl.ds(pl.multiple_of(j % 4 * B, B), B)
+        x = jnp.concatenate([ubuf[first, :], ubuf[second, :]], axis=0)
         hi, lo = split(x)
-        at = pl.multiple_of(j % 2 * B, B)
-        lu[j // 2, pl.ds(at, B), :] = hi
-        lu[j // 2, pl.ds(2 * B + at, B), :] = lo
-        at = pl.ds(pl.multiple_of(j * B, B), B)
+        uph[j // 4, at, :] = hi
+        upl[j // 4, at, :] = lo
         hi, lo = split(x.T)
-        for m in range(2):
-            lt[m, pl.ds(0, M), at] = hi[m * M:(m + 1) * M]
-            lt[m, pl.ds(M, M), at] = lo[m * M:(m + 1) * M]
+        tph[j // 4, :, at] = hi
+        tpl[j // 4, :, at] = lo
         return carry
 
     lax.fori_loop(0, 8, prep_natural, 0)
     own = rates[:, own_cols]
 
+    own_down = jnp.broadcast_to(own, (B, B)).T
+
     def prep_decay(i, carry):
         at = pl.ds(pl.multiple_of(i * B, B), B)
-        down = jnp.broadcast_to(rates[:, at], (B, B)).T
-        s = down + jnp.broadcast_to(own, (B, B))
-        rsum[at, :] = s
-        fd[at, :] = 1.0 / (1.0 + s)
+        half = pl.ds(pl.multiple_of(i % 4 * B, B), B)
+        total = jnp.broadcast_to(rates[:, at], (B, B)) + own_down
+        rsum[i // 4, :, half] = total
+        fd[i // 4, :, half] = 1.0 / (1.0 + total)
+        carried[i // 4, :, half] = cbuf[at, :].T
         return carry
 
     lax.fori_loop(0, 8, prep_decay, 0)
@@ -236,12 +233,11 @@
         force_a[h].start()
     lax.fori_loop(0, 8, prep_halves, 0)
 
-    def parts(m, e):
-        return pl.ds(m * M + e * E, E)
+    def share(e):
+        return pl.ds(pl.multiple_of(e * E, E), E)
 
     def s_copy(m, e, slot):
-        at = pl.ds(pl.multiple_of(m * M + e * E, E), E)
-        return remote(yref.at[at], srecv.at[m, slot], s_send.at[m, e], s_recv.at[m, slot], (e, me))
+        return remote(yref.at[m, share(e)], srecv.at[m, slot], s_send.at[m, e], s_recv.at[m, slot], (e, me))
 
     def c_copy(m, g, dev, slot):
         return remote(ssend.at[m, g], crecv.at[m, slot], c_send.at[m, g], c_recv.at[m, slot], (dev, me))
@@ -249,12 +245,12 @@
     def send_residual(m):
         for dx, dy in FAR_FIRST:
             s_copy(m, group_at(dx, dy), tm).start()
-        srecv[m, tm] = yref[pl.ds(pl.multiple_of(m * M + tm * E, E), E), :]
+        srecv[m, tm] = yref[m, share(tm), :]
 
     def scan_groups():
         for m in range(2):
-            cd = 1.0 / (1.0 + 2.0 * rsum[pl.ds(pl.multiple_of(m * M + tm * E, E), E), :])
-            corr = carried[m]
+            cd = 1.0 / (1.0 + 2.0 * rsum[m, share(tm), :])
+            corr = carried[m, share(tm), :]
             for d in range(1, TM):
                 e = lax.rem(tm + d, TM)
                 s_copy(m, e, e).wait_recv()
@@ -273,21 +269,21 @@
             for d in range(1, TM):
                 e = lax.rem(tm + d, TM)
                 c_copy(m, e, e, e).wait_recv()
-            at = pl.ds(m * M, M)
-            yref[at, :] = coefp[at, :] + crecv[m].reshape(M, B)
+            yref[m] = coefp[m] + crecv[m].reshape(B, M)
         for m in range(2):
             for d in range(1, TM):
                 e = lax.rem(tm + d, TM)
                 c_copy(m, e, e, tm).wait_send()
 
     def turn(k, carry):
-        def wide(x):
-            hi, lo = split(x)
-            return jnp.concatenate([hi, lo], axis=1)
-
-        def left_part(m, cols, ww):
-            a = dot(lt[m, :, cols], ww)
-            return a[:M, :B] + a[:M, B:] + a[M:, :B]
+        def left_half(h):
+            hi, lo = split(w[h].reshape(M, B).T)
+            return hi, jnp.concatenate([hi, lo], axis=0)
+
+        def left_part(h, m, hi, both):
+            cols = pl.ds(m * M, M)
+            a = dot(both, uph[h, :, cols])
+            return a[:B] + a[B:] + dot(hi, upl[h, :, cols])
 
         def waits(h, qs):
             def go(first):
@@ -297,14 +293,13 @@
             pl.when(k > 0)(lambda: go(False))
 
         waits(0, range(4))
-        ww = wide(w[0].reshape(M, B))
-        for m in range(2):
-            lacc[m] = left_part(m, pl.ds(0, M), ww)
+        hi, both = left_half(0)
+        for m in range(2):
+            lacc[m] = left_part(0, m, hi, both)
         waits(1, range(4))
-        ww = wide(w[1].reshape(M, B))
-        for m in range(2):
-            at = pl.ds(m * M, M)
-            yref[at, :] = fd[at, :] * (lacc[m] + left_part(m, pl.ds(M, M), ww))
+        hi, both = left_half(1)
+        for m in range(2):
+            yref[m] = fd[m] * (lacc[m] + left_part(1, m, hi, both))
             pl.when(k == 3)(lambda m=m: send_residual(m))
         pl.when(k == 0)(lambda: wait_w_sent(True))
         pl.when(k > 0)(lambda: wait_w_sent(False))
@@ -316,21 +311,22 @@
 
         pl.when(k == 3)(scan_groups)
 
-        yb[...] = wide(yref[...])
+        for m in range(2):
+            hi, lo = split(yref[m])
+            yb[pl.ds(0, B), pl.ds(m * M, M)] = hi
+            yb[pl.ds(B, B), pl.ds(m * M, M)] = lo
 
         for h in range(2):
-            for pr, chips in pairs:
-                a = dot(lu[h * 2 + pr], yb[...])
-                v = a[:2 * B, :B] + a[:2 * B, B:] + a[2 * B:, :B]
-                for i in range(4):
-                    sz[h, pr * 4 + i] = v[i * H:(i + 1) * H]
-                for zd in chips:
-                    for c in range(2):
-                        cp = z_copy(h, me, zd * 2 + c)
-                        if zd is zc:
-                            pl.when(core != c)(cp.start)
-                        else:
-                            cp.start()
+            a = dot(yb[...], tph[h])
+            v = a[:B] + a[B:] + dot(yb[pl.ds(0, B), :], tpl[h])
+            sz[h] = v.T.reshape(SPACE, H, B)
+            for zd in (far, partner(far), near, zc):
+                for c in range(2):
+                    cp = z_copy(h, me, zd * 2 + c)
+                    if zd is zc:
+                        pl.when(core != c)(cp.start)
+                    else:
+                        cp.start()
             z_in[h, me] = sz[h, me]
 
         for h in range(2):
@@ -398,7 +394,8 @@
     field = vm((B, N), F32)
     column = vm((N, B), F32)
     blocks = vm((2, SPACE, H, B), F32)
-    shares = vm((2, TM, E, B), F32)
+    pair = vm((2, B, M), F32)
+    shares = vm((2, TM, E, M), F32)
     basis = vm((N, N), BF16)
     two, eight, sixteen = dma((2,)), dma((2, SPACE)), dma((2, TM))
     fine, coarse = pl.pallas_call(
@@ -408,19 +405,19 @@
         out_specs=(vmem, vmem),
         scratch_shapes=[
             vm((N, N), F32), basis, basis, basis, basis,
-            vm((4, 4 * B, N), BF16), vm((2, N, N), BF16),
-            field, field, field, field, vm((2, E, B), F32),
-            vm((2, Q, N), F32), field, field, field, column, column, field,
+            vm((2, M, N), BF16), vm((2, M, N), BF16), vm((2, N, M), BF16), vm((2, N, M), BF16),
+            field, field, field, field, column, pair,
+            vm((2, Q, N), F32), field, field, field, pair, pair, field,
             blocks, blocks, blocks, blocks,
-            vm((2, B, N), BF16), vm((N, 2 * B), BF16),
-            column, column, column, vm((2, M, B), F32), field, shares, shares, shares,
-            dma((4,)), dma((6,)), two, two, two, two, two, two,
+            vm((2, B, N), BF16), vm((2 * B, N), BF16),
+            pair, pair, pair, pair, field, shares, shares, shares,
+            dma((4,)), dma((5,)), two, two, two, two, two, two,
             two, two, dma, dma, two, two,
             eight, eight, eight, eight, eight, eight,
             sixteen, sixteen, sixteen, sixteen,
         ],
         compiler_params=pltpu.CompilerParams(
-            collective_id=0, has_side_effects=True, vmem_limit_bytes=56000000
+            collective_id=0, has_side_effects=True, vmem_limit_bytes=55000000
         ),
         name="mgrit_cycle",
     )(

time: 124 us -> 120 us (0.968)
  Pallas kernels: 120 us -> 117 us
    pallas_call x1, Pallas kernels: 120 us -> 117 us  [on_device(): pl.pallas_call(kernel, out_shape=(jax.ShapeDtypeStruct((B, N), F32), jax....]
where the time goes in v4:
time: 120 us
  Pallas kernels  117 us (98%)
  local copies, waits for them, and re-layouts  2.27 us (2%)
    pallas_call x1, Pallas kernels, on_device(): pl.pallas_call(kernel, out_shape=(jax.ShapeDtypeStruct((B, N), F32), jax....  117 us

profile of v4, /device:TPU:1, one launch (start us, length us, event | category | flops | bytes accessed | tf_op | source)
XLA Modules:
  0.0 119.7 jit_solution(1664743092607896893)
XLA Ops:
  0.6 0.0 copy-start
  0.6 0.7 copy-done
  1.3 116.7 %mgrit_cycle.1 = (f32[128,1024]{1,0:T(8,128)S(1)}, f32[128,1024]{1,0:T(8,128)S(1)}) custom-call(f32[128,1024]{1,0:T(8,128)} %init_h.1, f32[128,1024]{1,0:T(8,128)} %bitcast.9, f32[128,1024]{1,0:T(8,128)} %bitcast.10, f32[128,1024]{1,0:T(8,128)} %bitcast.11, f32[1024,1024]{1,0:T(8,128)} %u_h.1, f32[1,1024]{1,0:T(1,128)S(1)} %bitcast.8, f32[1024,1024]{1,0:T(8,128)} %carried_h.1), custom_call_target="tpu_custom_call" | custom-call | tf_op jit(solution)/shard_map/mgrit_cycle/pallas_call | solution.py:401
  118.1 0.8 copy.11
  118.9 0.8 copy.12
Async XLA Ops:
  0.6 0.7 copy-start

commit v5 on v4

--- a/solution.py
+++ b/solution.py
@@ -49,7 +49,7 @@
     me = lax.axis_index("space")
     zc = me // 2
     core = me % 2
-    other = zc * 2 + (1 - core)
+    mine = core * 4 + zc
     nxt = lax.rem(tm + 1, TM)
     prv = lax.rem(tm + TM - 1, TM)
 
@@ -61,11 +61,7 @@
     def chip_of(q):
         return lax.rem(zc + q, 4)
 
-    def partner(chip):
-        return chip + 1 - 2 * (chip % 2)
-
-    far, near = chip_of(2), partner(zc)
-    pairs = ((far // 2, (far, partner(far))), (zc // 2, (near, zc)))
+    chips = (chip_of(2), chip_of(1), chip_of(3), zc)
 
     def group_at(dx, dy):
         return lax.rem(tm // 4 + dx, 4) * 4 + lax.rem(tm % 4 + dy, 4)
@@ -124,16 +120,20 @@
     def prep_natural(i, carry):
         at = pl.ds(pl.multiple_of(i * B, B), B)
         hi, lo = split(ubuf[at, :])
-        uh[at, :] = hi
-        ul[at, :] = lo
+        for s in range(SPACE):
+            old, new = slice(s * B, (s + 1) * B), pl.ds((s % 2 * 4 + s // 2) * B, B)
+            uh[at, new] = hi[:, old]
+            ul[at, new] = lo[:, old]
         hi, lo = split(ubuf[at, :].T)
-        th[:, at] = hi
-        tl[:, at] = lo
+        for s in range(SPACE):
+            old, new = slice(s * B, (s + 1) * B), pl.ds((s % 2 * 4 + s // 2) * B, B)
+            th[new, at] = hi[old]
+            tl[new, at] = lo[old]
         return carry
 
     def prep_halves(j, carry):
-        row = (j % 4) * 256 + (j // 4) * H
-        first, second = pl.ds(pl.multiple_of(row, H), H), pl.ds(pl.multiple_of(row + B, H), H)
+        row = (j % 2 * 4 + j % 4 // 2) * B + (j // 4) * H
+        first, second = pl.ds(pl.multiple_of(row, H), H), pl.ds(pl.multiple_of(row + 2 * B, H), H)
         at = pl.ds(pl.multiple_of(j % 4 * B, B), B)
         x = jnp.concatenate([ubuf[first, :], ubuf[second, :]], axis=0)
         hi, lo = split(x)
@@ -162,60 +162,57 @@
 
     keep, give = pl.ds(0, Q), pl.ds(Q, Q)
 
-    def w_copies(h, s, d, first):
+    def w_copies(h, s, chip, c, first):
+        d, dev = c * 4 + chip, chip * 2 + c
         if not first:
-            return (remote(sw.at[h, d], w.at[h, s], w_send.at[h, d], w_recv.at[h, s], (tm, d)),)
+            return (remote(sw.at[h, d], w.at[h, s], w_send.at[h, d], w_recv.at[h, s], (tm, dev)),)
         return (
-            remote(sw.at[h, d, keep], w.at[h, s, keep], w_send.at[h, d], w_recv.at[h, s], (tm, d)),
-            remote(sw.at[h, d, give], w.at[h, s, give], wb_send.at[h, d], wb_recv.at[h, s], (nxt, d)),
+            remote(sw.at[h, d, keep], w.at[h, s, keep], w_send.at[h, d], w_recv.at[h, s], (tm, dev)),
+            remote(sw.at[h, d, give], w.at[h, s, give], wb_send.at[h, d], wb_recv.at[h, s], (nxt, dev)),
         )
 
-    def z_copy(h, s, d):
-        return remote(sz.at[h, d], z_in.at[h, s], z_send.at[h, d], z_recv.at[h, s], (tm, d))
+    def z_copy(h, s, chip, c):
+        d = c * 4 + chip
+        return remote(sz.at[h, d], z_in.at[h, s], z_send.at[h, d], z_recv.at[h, s], (tm, chip * 2 + c))
+
+    def unless_mine(chip, c, act):
+        if chip is zc:
+            pl.when(core != c)(act)
+        else:
+            act()
 
     def right_send(h, first):
-        for pr, chips in pairs:
-            cols = pl.ds(pl.multiple_of(pr * M, M), M)
+        for c in range(2):
+            cols = pl.ds(c * M, M)
             a = dot(xs[h], uh[:, cols])
             p = a[:H] + a[H:] + dot(xs[h, pl.ds(0, H), :], ul[:, cols])
             for i in range(4):
-                sw[h, pr * 4 + i] = p[:, i * B:(i + 1) * B]
-            for zd in chips:
-                for c in range(2):
-                    copies = w_copies(h, me, zd * 2 + c, first)
-                    if zd is zc:
-                        pl.when(core != c)(copies[0].start)
-                    else:
-                        copies[0].start()
-                    if first:
-                        copies[1].start()
+                sw[h, c * 4 + i] = p[:, i * B:(i + 1) * B]
+            for chip in chips:
+                copies = w_copies(h, mine, chip, c, first)
+                unless_mine(chip, c, copies[0].start)
+                if first:
+                    copies[1].start()
         if first:
-            w[h, me, keep] = sw[h, me, keep]
+            w[h, mine, keep] = sw[h, mine, keep]
         else:
-            w[h, me] = sw[h, me]
-
-    def wait_w(h, q, first):
-        if q:
-            zs = chip_of(q)
-            for s in (zs * 2, zs * 2 + 1):
-                for c in w_copies(h, s, s, first):
-                    c.wait_recv()
-        else:
-            for c in w_copies(h, other, other, first):
-                c.wait_recv()
+            w[h, mine] = sw[h, mine]
+
+    def wait_w(h, c, first):
+        for chip in chips:
+            copies = w_copies(h, c * 4 + chip, chip, c, first)
+            unless_mine(chip, c, copies[0].wait_recv)
             if first:
-                w_copies(h, me, me, True)[1].wait_recv()
+                copies[1].wait_recv()
 
     def wait_w_sent(first):
         for h in range(2):
-            for q in (1, 2, 3):
-                for i in range(2):
-                    for c in w_copies(h, me, chip_of(q) * 2 + i, first):
-                        c.wait_send()
-            for c in w_copies(h, me, other, first):
-                c.wait_send()
-            if first:
-                w_copies(h, me, me, True)[1].wait_send()
+            for c in range(2):
+                for chip in chips:
+                    copies = w_copies(h, mine, chip, c, first)
+                    unless_mine(chip, c, copies[0].wait_send)
+                    if first:
+                        copies[1].wait_send()
 
     def put_xs(h, x):
         hi, lo = split(x)
@@ -276,31 +273,32 @@
                 c_copy(m, e, e, tm).wait_send()
 
     def turn(k, carry):
-        def left_half(h):
-            hi, lo = split(w[h].reshape(M, B).T)
+        def left_rows(h, c):
+            hi, lo = split(w[h, pl.ds(c * 4, 4)].reshape(2 * B, B).T)
             return hi, jnp.concatenate([hi, lo], axis=0)
 
-        def left_part(h, m, hi, both):
+        def left_part(h, rows, m, hi, both):
             cols = pl.ds(m * M, M)
-            a = dot(both, uph[h, :, cols])
-            return a[:B] + a[B:] + dot(hi, upl[h, :, cols])
-
-        def waits(h, qs):
-            def go(first):
-                for q in qs:
-                    wait_w(h, q, first)
-            pl.when(k == 0)(lambda: go(True))
-            pl.when(k > 0)(lambda: go(False))
-
-        waits(0, range(4))
-        hi, both = left_half(0)
-        for m in range(2):
-            lacc[m] = left_part(0, m, hi, both)
-        waits(1, range(4))
-        hi, both = left_half(1)
-        for m in range(2):
-            yref[m] = fd[m] * (lacc[m] + left_part(1, m, hi, both))
-            pl.when(k == 3)(lambda m=m: send_residual(m))
+            a = dot(both, uph[h, rows, cols])
+            return a[:B] + a[B:] + dot(hi, upl[h, rows, cols])
+
+        def waits(h, c):
+            pl.when(k == 0)(lambda: wait_w(h, c, True))
+            pl.when(k > 0)(lambda: wait_w(h, c, False))
+
+        for n, (h, c) in enumerate(((0, 0), (0, 1), (1, 0), (1, 1))):
+            waits(h, c)
+            rows = pl.ds(c * 2 * B, 2 * B)
+            hi, both = left_rows(h, c)
+            for m in range(2):
+                v = left_part(h, rows, m, hi, both)
+                if n:
+                    v += lacc[m]
+                if n < 3:
+                    lacc[m] = v
+                else:
+                    yref[m] = fd[m] * v
+                    pl.when(k == 3)(lambda m=m: send_residual(m))
         pl.when(k == 0)(lambda: wait_w_sent(True))
         pl.when(k > 0)(lambda: wait_w_sent(False))
 
@@ -320,24 +318,24 @@
             a = dot(yb[...], tph[h])
             v = a[:B] + a[B:] + dot(yb[pl.ds(0, B), :], tpl[h])
             sz[h] = v.T.reshape(SPACE, H, B)
-            for zd in (far, partner(far), near, zc):
-                for c in range(2):
-                    cp = z_copy(h, me, zd * 2 + c)
-                    if zd is zc:
-                        pl.when(core != c)(cp.start)
-                    else:
-                        cp.start()
-            z_in[h, me] = sz[h, me]
+            for c in range(2):
+                for chip in chips:
+                    unless_mine(chip, c, z_copy(h, mine, chip, c).start)
+            z_in[h, mine] = sz[h, mine]
 
         for h in range(2):
-            for q in range(4):
-                zs = chip_of(q)
-                for s in (zs * 2, zs * 2 + 1) if q else (other,):
-                    z_copy(h, s, s).wait_recv()
             rows = rows_of(h)
-            hi, lo = split(jnp.concatenate([z_in[h, s] for s in range(SPACE)], axis=1))
-            a = dot(jnp.concatenate([hi, lo], axis=0), th[...])
-            facc[rows, :] = a[:H] + a[H:] + dot(hi, tl[...])
+            for c in range(2):
+                for chip in chips:
+                    unless_mine(chip, c, z_copy(h, c * 4 + chip, chip, c).wait_recv)
+                depth = pl.ds(c * M, M)
+                hi, lo = split(jnp.concatenate([z_in[h, c * 4 + i] for i in range(4)], axis=1))
+                a = dot(jnp.concatenate([hi, lo], axis=0), th[depth, :])
+                v = a[:H] + a[H:] + dot(hi, tl[depth, :])
+                if c:
+                    facc[rows, :] += v
+                else:
+                    facc[rows, :] = v
 
             @pl.when(k == 3)
             def _():
@@ -374,10 +372,9 @@
                 right_send(h, False)
 
         for h in range(2):
-            for q in (1, 2, 3):
-                for c in range(2):
-                    z_copy(h, me, chip_of(q) * 2 + c).wait_send()
-            z_copy(h, me, other).wait_send()
+            for c in range(2):
+                for chip in chips:
+                    unless_mine(chip, c, z_copy(h, mine, chip, c).wait_send)
         return carry
 
     lax.fori_loop(0, 5, turn, 0)

time: 120 us -> 116 us (0.967)
  Pallas kernels: 117 us -> 113 us
    pallas_call x1, Pallas kernels: 117 us -> 113 us  [on_device(): pl.pallas_call(kernel, out_shape=(jax.ShapeDtypeStruct((B, N), F32), jax....]
where the time goes in v5:
time: 116 us
  Pallas kernels  113 us (97%)
  local copies, waits for them, and re-layouts  2.27 us (2%)
    pallas_call x1, Pallas kernels, on_device(): pl.pallas_call(kernel, out_shape=(jax.ShapeDtypeStruct((B, N), F32), jax....  113 us

profile of v5, /device:TPU:1, one launch (start us, length us, event | category | flops | bytes accessed | tf_op | source)
XLA Modules:
  0.0 115.7 jit_solution(9296202108236991981)
XLA Ops:
  0.6 0.0 copy-start
  0.6 0.7 copy-done
  1.3 112.8 %mgrit_cycle.1 = (f32[128,1024]{1,0:T(8,128)S(1)}, f32[128,1024]{1,0:T(8,128)S(1)}) custom-call(f32[128,1024]{1,0:T(8,128)} %init_h.1, f32[128,1024]{1,0:T(8,128)} %bitcast.9, f32[128,1024]{1,0:T(8,128)} %bitcast.10, f32[128,1024]{1,0:T(8,128)} %bitcast.11, f32[1024,1024]{1,0:T(8,128)} %u_h.1, f32[1,1024]{1,0:T(1,128)S(1)} %bitcast.8, f32[1024,1024]{1,0:T(8,128)} %carried_h.1), custom_call_target="tpu_custom_call" | custom-call | tf_op jit(solution)/shard_map/mgrit_cycle/pallas_call | solution.py:398
  114.1 0.8 copy.11
  114.9 0.8 copy.12
Async XLA Ops:
  0.6 0.7 copy-start

commit v6 on v5

v6 whole, which is shorter than its diff:
```python
import jax
import jax.numpy as jnp
from jax import lax
from jax.experimental import pallas as pl
from jax.experimental.pallas import tpu as pltpu
from jax.sharding import PartitionSpec as P

MESH = pl.DeviceIdType.MESH
F32 = jnp.float32
BF16 = jnp.bfloat16
TM = 16
SPACE = 8
N = 1024
B = 128
H = B // 2
Q = H // 2
R = Q // 2
M = N // 2
E = B // TM
FAR_FIRST = sorted(
    ((x, y) for x in range(4) for y in range(4) if x or y), key=lambda t: -min(t[0], 4 - t[0]) - min(t[1], 4 - t[1])
)


def dot(a, b):
    return jnp.dot(a, b, preferred_element_type=F32)


def react(field):
    return field + 0.5 * jnp.tanh(field)


def split(x):
    hi = x.astype(BF16)
    return hi, (x - hi.astype(F32)).astype(BF16)


def kernel(
    init_h, guess_h, ff_h, fc_h, u_h, rates, carried_h,
    fs_o, cs_o,
    ubuf, uh, ul, th, tl, uph, upl, tph, tpl, init, guess, ff, fc, cbuf, carried,
    ga, ffn, nrf, nrfn, coef, coefp, csb,
    sw, w, sz, z_in, xs, yb, fd, rsum, yref, lacc, facc, srecv, ssend, crecv,
    u_sem, loc_sem, ga_send, ga_recv, fb_send, fb_recv, fa_send, fa_recv,
    nr_send, nr_recv, co_send, co_recv, cs_send, cs_recv,
    w_send, w_recv, wb_send, wb_recv, z_send, z_recv,
    s_send, s_recv, c_send, c_recv,
):
    tm = lax.axis_index("tm")
    me = lax.axis_index("space")
    zc = me // 2
    core = me % 2
    mine = core * 4 + zc
    nxt = lax.rem(tm + 1, TM)
    prv = lax.rem(tm + TM - 1, TM)

    def remote(src, dst, ss, rs, dev):
        return pltpu.make_async_remote_copy(
            src_ref=src, dst_ref=dst, send_sem=ss, recv_sem=rs, device_id=dev, device_id_type=MESH
        )

    def chip_of(q):
        return lax.rem(zc + q, 4)

    chips = (chip_of(2), chip_of(1), chip_of(3), zc)

    def group_at(dx, dy):
        return lax.rem(tm // 4 + dx, 4) * 4 + lax.rem(tm % 4 + dy, 4)

    u_copies = [
        pltpu.make_async_copy(u_h.at[pl.ds(i * 256, 256)], ubuf.at[pl.ds(i * 256, 256)], u_sem.at[i])
        for i in range(4)
    ]
    own_cols = pl.ds(pl.multiple_of(me * B, B), B)
    loads = [
        pltpu.make_async_copy(init_h, init, loc_sem.at[0]),
        pltpu.make_async_copy(guess_h, guess, loc_sem.at[1]),
        pltpu.make_async_copy(ff_h, ff, loc_sem.at[2]),
        pltpu.make_async_copy(fc_h, fc, loc_sem.at[3]),
        pltpu.make_async_copy(carried_h.at[:, own_cols], cbuf, loc_sem.at[4]),
    ]
    for c in u_copies + loads:
        c.start()

    barrier = pltpu.get_barrier_semaphore()
    count = 0
    for d in range(1, SPACE):
        for t in (tm, nxt, prv):
            pl.semaphore_signal(barrier, inc=1, device_id=(t, lax.rem(me + d, SPACE)), device_id_type=MESH)
            count += 1
    for d in range(1, TM):
        pl.semaphore_signal(barrier, inc=1, device_id=(lax.rem(tm + d, TM), me), device_id_type=MESH)
        count += 1

    for c in loads:
        c.wait()
    pl.semaphore_wait(barrier, count)

    def part_a(i):
        return pl.ds(i * Q, R)

    def part_b(i):
        return pl.ds(i * Q + R, R)

    def rows_of(h):
        return pl.ds(h * H, H)

    guess_shift = [remote(guess.at[part_a(i)], ga.at[i], ga_send.at[i], ga_recv.at[i], (nxt, me)) for i in range(4)]
    force_b = [remote(ff.at[part_b(i)], ffn.at[part_b(i)], fb_send.at[i], fb_recv.at[i], (prv, me)) for i in range(4)]
    force_a = [remote(ff.at[part_a(i)], ffn.at[part_a(i)], fa_send.at[i], fa_recv.at[i], (prv, me)) for i in range(4)]
    nrf_shift = [remote(nrf.at[rows_of(h)], nrfn.at[rows_of(h)], nr_send.at[h], nr_recv.at[h], (prv, me)) for h in range(2)]
    coef_shift = remote(coef, coefp, co_send, co_recv, (nxt, me))
    cs_shift = [remote(csb.at[rows_of(h)], cs_o.at[rows_of(h)], cs_send.at[h], cs_recv.at[h], (prv, me)) for h in range(2)]
    for i in range(4):
        guess_shift[i].start()
        force_b[i].start()

    for c in u_copies:
        c.wait()

    def prep_natural(i, carry):
        at = pl.ds(pl.multiple_of(i * B, B), B)
        hi, lo = split(ubuf[at, :])
        for s in range(SPACE):
            old, new = slice(s * B, (s + 1) * B), pl.ds((s % 2 * 4 + s // 2) * B, B)
            uh[at, new] = hi[:, old]
            ul[at, new] = lo[:, old]
        hi, lo = split(ubuf[at, :].T)
        for s in range(SPACE):
            for p in range(2):
                old = slice(s * B + p * H, s * B + (p + 1) * H)
                new = pl.ds(p * M + (s % 2 * 4 + s // 2) * H, H)
                th[new, at] = hi[old]
                tl[new, at] = lo[old]
        return carry

    def prep_halves(j, carry):
        row = j % 4 // 2 * B + j // 4 * H + j % 2 * Q
        at = pl.ds(pl.multiple_of(j % 4 * B, B), B)
        x = jnp.concatenate([ubuf[pl.ds(pl.multiple_of(row + i * 2 * B, Q), Q), :] for i in range(4)], axis=0)
        hi, lo = split(x)
        uph[j // 4, at, :] = hi
        upl[j // 4, at, :] = lo
        hi, lo = split(x.T)
        tph[j // 4, :, at] = hi
        tpl[j // 4, :, at] = lo
        return carry

    lax.fori_loop(0, 8, prep_natural, 0)
    own = rates[:, own_cols]

    own_down = jnp.broadcast_to(own, (B, B)).T

    def prep_decay(i, carry):
        at = pl.ds(pl.multiple_of(i * B, B), B)
        half = pl.ds(pl.multiple_of(i % 4 * B, B), B)
        total = jnp.broadcast_to(rates[:, at], (B, B)) + own_down
        rates_in = 1.0 / (1.0 + total)
        before = cbuf[at, :].T
        for p in range(2):
            own_part = slice(p * H, (p + 1) * H)
            rsum[p, i // 4, :, half] = total[own_part]
            fd[p, i // 4, :, half] = rates_in[own_part]
            carried[p, i // 4, :, half] = before[own_part]
        return carry

    lax.fori_loop(0, 8, prep_decay, 0)

    keep, give = pl.ds(0, R), pl.ds(R, R)
    left = lax.broadcasted_iota(jnp.int32, (Q, B), 1) < H

    def w_copies(h, p, s, chip, c, first):
        d, dev, n = c * 4 + chip, chip * 2 + c, h * 2 + p
        if not first:
            return (remote(sw.at[n, d], w.at[n, s], w_send.at[n, d], w_recv.at[n, s], (tm, dev)),)
        return (
            remote(sw.at[n, d, keep], w.at[n, s, keep], w_send.at[n, d], w_recv.at[n, s], (tm, dev)),
            remote(sw.at[n, d, give], w.at[n, s, give], wb_send.at[n, d], wb_recv.at[n, s], (nxt, dev)),
        )

    def z_copy(h, p, s, chip, c):
        d, n = c * 4 + chip, h * 2 + p
        return remote(sz.at[n, d], z_in.at[n, s], z_send.at[n, d], z_recv.at[n, s], (tm, chip * 2 + c))

    def unless_mine(chip, c, act):
        if chip is zc:
            pl.when(core != c)(act)
        else:
            act()

    def w_start(h, p, c, first):
        for chip in chips:
            copies = w_copies(h, p, mine, chip, c, first)
            unless_mine(chip, c, copies[0].start)
            if first:
                copies[1].start()

    def right_send(h, first):
        for c in range(2):
            cols = pl.ds(c * M, M)
            a = dot(xs[h], uh[:, cols])
            p = a[:H] + a[H:] + dot(xs[h, pl.ds(0, H), :], ul[:, cols])
            for i in range(4):
                block = p[:, i * B:(i + 1) * B]
                turned = pltpu.roll(block, H, 1)
                sw[h * 2, c * 4 + i] = jnp.where(left, block[:Q], turned[Q:])
                sw[h * 2 + 1, c * 4 + i] = jnp.where(left, turned[:Q], block[Q:])
            for n in ((h, 0, c), (h, 1, c)) if h == 0 else ((h, 0, c),):
                w_start(*n, first)
        if h:
            for c in range(2):
                w_start(h, 1, c, first)
        for p in range(2):
            if first:
                w[h * 2 + p, mine, keep] = sw[h * 2 + p, mine, keep]
            else:
                w[h * 2 + p, mine] = sw[h * 2 + p, mine]

    def wait_w(h, p, c, first):
        for chip in chips:
            copies = w_copies(h, p, c * 4 + chip, chip, c, first)
            unless_mine(chip, c, copies[0].wait_recv)
            if first:
                copies[1].wait_recv()

    def wait_w_sent(first):
        for h in range(2):
            for p in range(2):
                for c in range(2):
                    for chip in chips:
                        copies = w_copies(h, p, mine, chip, c, first)
                        unless_mine(chip, c, copies[0].wait_send)
                        if first:
                            copies[1].wait_send()

    def put_xs(h, x):
        hi, lo = split(x)
        xs[h, pl.ds(0, H), :] = hi
        xs[h, pl.ds(H, H), :] = lo

    for h in range(2):
        x = []
        for i in (2 * h, 2 * h + 1):
            guess_shift[i].wait_recv()
            x.append(react(jnp.where(tm == 0, init[part_a(i), :], ga[i])) + ff[part_a(i), :])
            force_b[i].wait_recv()
            x.append(react(jnp.where(tm == TM - 1, init[part_b(i), :], guess[part_b(i), :])) + ffn[part_b(i), :])
        put_xs(h, jnp.concatenate(x, axis=0))
        right_send(h, True)
    for i in range(4):
        force_a[i].start()
    lax.fori_loop(0, 8, prep_halves, 0)

    def put_yb(p, m, y):
        hi, lo = split(y)
        yb[p, pl.ds(0, H), pl.ds(m * M, M)] = hi
        yb[p, pl.ds(H, H), pl.ds(m * M, M)] = lo

    def share(e):
        return pl.ds(pl.multiple_of(e // 2 * E, E), E)

    def s_copy(p, e, slot):
        return remote(yref.at[p, e % 2, share(e)], srecv.at[p, slot], s_send.at[p, e], s_recv.at[p, slot], (e, me))

    def c_copy(p, g, dev, slot):
        return remote(
            ssend.at[p, g], crecv.at[p, slot // 2, slot % 2], c_send.at[p, g], c_recv.at[p, slot], (dev, me)
        )

    def send_residual(p):
        for dx, dy in FAR_FIRST:
            s_copy(p, group_at(dx, dy), tm).start()
        srecv[p, tm] = yref[p, tm % 2, share(tm), :]

    def scan_groups():
        for p in range(2):
            cd = 1.0 / (1.0 + 2.0 * rsum[p, tm % 2, share(tm), :])
            corr = carried[p, tm % 2, share(tm), :]
            for d in range(1, TM):
                e = lax.rem(tm + d, TM)
                s_copy(p, e, e).wait_recv()
            for g in range(TM):
                corr = cd * corr + srecv[p, (g + TM - 1) % TM]
                ssend[p, (g + 1) % TM] = corr
            for dx, dy in FAR_FIRST:
                dest = group_at(dx, dy)
                c_copy(p, dest, dest, tm).start()
            crecv[p, tm // 2, tm % 2] = ssend[p, tm]
        coef_shift.wait()

    def take_correction(p):
        for d in range(1, TM):
            e = lax.rem(tm + d, TM)
            c_copy(p, e, e, e).wait_recv()
        for m in range(2):
            put_yb(p, m, coefp[p, m] + crecv[p, :, m].reshape(H, M))

    def scan_sent():
        for p in range(2):
            for d in range(1, TM):
                e = lax.rem(tm + d, TM)
                s_copy(p, e, tm).wait_send()
                c_copy(p, e, e, tm).wait_send()

    def left_inverse(h, p):
        a = dot(yb[p], tph[h])
        v = a[:H] + a[H:] + dot(yb[p, pl.ds(0, H), :], tpl[h])
        for c in range(2):
            at = c * 2 * B
            both = jnp.concatenate([v[:, at:at + B], v[:, at + B:at + 2 * B]], axis=0)
            sz[h * 2 + p, pl.ds(c * 4, 4)] = both.T.reshape(4, Q, B)
        z_start(h, p)

    def z_start(h, p):
        for c in range(2):
            for chip in chips:
                unless_mine(chip, c, z_copy(h, p, mine, chip, c).start)
        z_in[h * 2 + p, mine] = sz[h * 2 + p, mine]

    def turn(k, carry):
        def waits(h, p, c):
            pl.when(k == 0)(lambda: wait_w(h, p, c, True))
            pl.when(k > 0)(lambda: wait_w(h, p, c, False))

        def left_rows(h, p, c):
            t = w[h * 2 + p, pl.ds(c * 4, 4)].reshape(B, B).T
            return [t[:H], t[H:]]

        def left_part(h, rows, x):
            hi, lo = split(jnp.concatenate(x, axis=1))
            a = dot(jnp.concatenate([hi, lo], axis=0), uph[h, rows, :])
            return a[:H] + a[H:] + dot(hi, upl[h, rows, :])

        def finish(p):
            for c in range(2):
                waits(1, p, c)
                v = lacc[p] + left_part(1, pl.ds(c * 2 * B, 2 * B), left_rows(1, p, c))
                if c == 0:
                    lacc[p] = v
                else:
                    for m in range(2):
                        y = fd[p, m] * v[:, m * M:(m + 1) * M]
                        yref[p, m] = y
                        put_yb(p, m, y)

        for p in range(2):
            waits(0, p, 0)
            waits(0, p, 1)
            lacc[p] = left_part(0, pl.ds(0, M), left_rows(0, p, 0) + left_rows(0, p, 1))
        finish(0)
        pl.when(k == 3)(lambda: send_residual(0))
        pl.when(k != 3)(lambda: left_inverse(0, 0))
        finish(1)

        @pl.when(k == 3)
        def _():
            send_residual(1)
            scan_groups()
            take_correction(0)
            left_inverse(0, 0)
            take_correction(1)
            scan_sent()

        left_inverse(0, 1)
        left_inverse(1, 0)
        left_inverse(1, 1)

        pl.when(k == 0)(lambda: wait_w_sent(True))
        pl.when(k > 0)(lambda: wait_w_sent(False))

        @pl.when(k == 1)
        def _():
            coef[...] = yref[...]
            coef_shift.start()

        for h in range(2):
            rows = rows_of(h)
            for p in range(2):
                for c in range(2):
                    for chip in chips:
                        unless_mine(chip, c, z_copy(h, p, c * 4 + chip, chip, c).wait_recv)
                x = []
                for i in range(0, SPACE, 2):
                    one, two = z_in[h * 2 + p, i], z_in[h * 2 + p, i + 1]
                    x.append(jnp.concatenate(
                        [jnp.where(left, one, pltpu.roll(two, H, 1)), jnp.where(left, pltpu.roll(one, H, 1), two)], axis=0
                    ))
                depth = pl.ds(p * M, M)
                hi, lo = split(jnp.concatenate(x, axis=1))
                a = dot(jnp.concatenate([hi, lo], axis=0), th[depth, :])
                v = a[:H] + a[H:] + dot(hi, tl[depth, :])
                if p:
                    facc[rows, :] += v
                else:
                    facc[rows, :] = v

            @pl.when(k == 3)
            def _():
                csb[rows, :] = facc[rows, :]
                cs_shift[h].start()

            @pl.when(k < 4)
            def _():
                restart = ((k == 1) & (tm == TM - 1)) | ((k == 3) & (tm == 0))
                facc[rows, :] = react(jnp.where(restart, init[rows, :], facc[rows, :]))

                @pl.when(k == 0)
                def _():
                    nrf[rows, :] = facc[rows, :]
                    nrf_shift[h].start()
                    facc[rows, :] += fc[rows, :]

                @pl.when(k == 1)
                def _():
                    for i in (2 * h, 2 * h + 1):
                        force_b[i].wait_send()
                        force_a[i].wait()
                    facc[rows, :] += ffn[rows, :]

                @pl.when(k == 2)
                def _():
                    nrf_shift[h].wait()
                    facc[rows, :] -= nrfn[rows, :]

                @pl.when(k == 3)
                def _():
                    facc[rows, :] += ff[rows, :]

                put_xs(h, facc[rows, :])
                right_send(h, False)

        for h in range(2):
            for p in range(2):
                for c in range(2):
                    for chip in chips:
                        unless_mine(chip, c, z_copy(h, p, mine, chip, c).wait_send)
        return carry

    lax.fori_loop(0, 5, turn, 0)
    fs_o[...] = facc[...]
    for i in range(4):
        guess_shift[i].wait_send()
    for h in range(2):
        cs_shift[h].wait()


def on_device(initial_state, guess_coarse, force_fine, force_coarse, eigen_basis, eigen_rates, carried_correction):
    vm, dma = pltpu.VMEM, pltpu.SemaphoreType.DMA
    hbm = pl.BlockSpec(memory_space=pl.ANY)
    vmem = pl.BlockSpec(memory_space=pltpu.VMEM)
    field = vm((B, N), F32)
    column = vm((N, B), F32)
    blocks = vm((4, SPACE, Q, B), F32)
    pair = vm((2, 2, H, M), F32)
    shares = vm((2, TM, E, M), F32)
    basis = vm((N, N), BF16)
    two, four, eight, sixteen = dma((2,)), dma((4,)), dma((4, SPACE)), dma((2, TM))
    fine, coarse = pl.pallas_call(
        kernel,
        out_shape=(jax.ShapeDtypeStruct((B, N), F32), jax.ShapeDtypeStruct((B, N), F32)),
        in_specs=[hbm] * 5 + [vmem, hbm],
        out_specs=(vmem, vmem),
        scratch_shapes=[
            vm((N, N), F32), basis, basis, basis, basis,
            vm((2, M, N), BF16), vm((2, M, N), BF16), vm((2, N, M), BF16), vm((2, N, M), BF16),
            field, field, field, field, column, pair,
            vm((4, R, N), F32), field, field, field, pair, pair, field,
            blocks, blocks, blocks, blocks,
            vm((2, B, N), BF16), vm((2, B, N), BF16),
            pair, pair, pair, vm((2, H, N), F32), field, shares, shares, vm((2, TM // 2, 2, E, M), F32),
            dma((4,)), dma((5,)), four, four, four, four, four, four,
            two, two, dma, dma, two, two,
            eight, eight, eight, eight, eight, eight,
            sixteen, sixteen, sixteen, sixteen,
        ],
        compiler_params=pltpu.CompilerParams(
            collective_id=0, has_side_effects=True, vmem_limit_bytes=55000000
        ),
        name="mgrit_cycle",
    )(
        initial_state, guess_coarse[0], force_fine[0], force_coarse[0],
        eigen_basis, eigen_rates[None, :], carried_correction,
    )
    return fine[None], coarse[None]


def solution(mesh):
    rows = P("tm", "space", None)
    return jax.shard_map(
        on_device,
        mesh=mesh,
        in_specs=(P("space", None), rows, rows, rows, P(), P(), P()),
        out_specs=(rows, rows),
        check_vma=False,
    )
```

time: 116 us -> 113 us (0.974)
  Pallas kernels: 113 us -> 109 us
    pallas_call x1, Pallas kernels: 113 us -> 109 us  [on_device(): pl.pallas_call(kernel, out_shape=(jax.ShapeDtypeStruct((B, N), F32), jax....]
where the time goes in v6:
time: 113 us; the launch traced here: 112 us
  Pallas kernels  109 us (96%)
  local copies, waits for them, and re-layouts  2.27 us (2%)
    pallas_call x1, Pallas kernels, on_device(): pl.pallas_call(kernel, out_shape=(jax.ShapeDtypeStruct((B, N), F32), jax....  109 us
    unnamed x4, local copies, waits for them, and re-layouts  2.27 us

profile of v6, /device:TPU:1, one launch (start us, length us, event | category | flops | bytes accessed | tf_op | source)
XLA Modules:
  0.0 112.4 jit_solution(17165878742259737601)
XLA Ops:
  0.6 0.0 copy-start
  0.6 0.7 copy-done
  1.3 109.5 %mgrit_cycle.1 = (f32[128,1024]{1,0:T(8,128)S(1)}, f32[128,1024]{1,0:T(8,128)S(1)}) custom-call(f32[128,1024]{1,0:T(8,128)} %init_h.1, f32[128,1024]{1,0:T(8,128)} %bitcast.9, f32[128,1024]{1,0:T(8,128)} %bitcast.10, f32[128,1024]{1,0:T(8,128)} %bitcast.11, f32[1024,1024]{1,0:T(8,128)} %u_h.1, f32[1,1024]{1,0:T(1,128)S(1)} %bitcast.8, f32[1024,1024]{1,0:T(8,128)} %carried_h.1), custom_call_target="tpu_custom_call" | custom-call | tf_op jit(solution)/shard_map/mgrit_cycle/pallas_call | solution.py:458
  110.8 0.8 copy.11
  111.6 0.8 copy.12
Async XLA Ops:
  0.6 0.7 copy-start

commit v7 on v6

--- a/solution.py
+++ b/solution.py
@@ -44,7 +44,7 @@
     u_sem, loc_sem, ga_send, ga_recv, fb_send, fb_recv, fa_send, fa_recv,
     nr_send, nr_recv, co_send, co_recv, cs_send, cs_recv,
     w_send, w_recv, wb_send, wb_recv, z_send, z_recv,
-    s_send, s_recv, c_send, c_recv,
+    s_send, s_recv, c_send, c_recv, up_sem, down_sem,
 ):
     tm = lax.axis_index("tm")
     me = lax.axis_index("space")
@@ -83,14 +83,10 @@
         c.start()
 
     barrier = pltpu.get_barrier_semaphore()
-    count = 0
-    for d in range(1, SPACE):
-        for t in (tm, nxt, prv):
-            pl.semaphore_signal(barrier, inc=1, device_id=(t, lax.rem(me + d, SPACE)), device_id_type=MESH)
-            count += 1
-    for d in range(1, TM):
-        pl.semaphore_signal(barrier, inc=1, device_id=(lax.rem(tm + d, TM), me), device_id_type=MESH)
-        count += 1
+    near = [(tm, lax.rem(me + d, SPACE)) for d in range(1, SPACE)] + [(nxt, me), (prv, me)]
+    count = len(near)
+    for dev in near:
+        pl.semaphore_signal(barrier, inc=1, device_id=dev, device_id_type=MESH)
 
     for c in loads:
         c.wait()
@@ -118,13 +114,19 @@
     for c in u_copies:
         c.wait()
 
-    def prep_natural(i, carry):
-        at = pl.ds(pl.multiple_of(i * B, B), B)
-        hi, lo = split(ubuf[at, :])
-        for s in range(SPACE):
-            old, new = slice(s * B, (s + 1) * B), pl.ds((s % 2 * 4 + s // 2) * B, B)
-            uh[at, new] = hi[:, old]
-            ul[at, new] = lo[:, old]
+    left_half = lax.broadcasted_iota(jnp.int32, (B, B), 1) < H
+
+    def prep_natural(n, carry):
+        at = pl.ds(pl.multiple_of(n * B, B), B)
+        x = ubuf[at, :]
+        for i in range(4):
+            low = (i % 2 * 4 + i // 2) * B
+            one, two = x[:, low:low + B], x[:, low + 2 * B:low + 3 * B]
+            halves = (jnp.where(left_half, one, pltpu.roll(two, H, 1)), jnp.where(left_half, pltpu.roll(one, H, 1), two))
+            for p in range(2):
+                hi, lo = split(halves[p])
+                uh[at, pl.ds(p * M + i * B, B)] = hi
+                ul[at, pl.ds(p * M + i * B, B)] = lo
         hi, lo = split(ubuf[at, :].T)
         for s in range(SPACE):
             for p in range(2):
@@ -196,21 +198,17 @@
                 copies[1].start()
 
     def right_send(h, first):
-        for c in range(2):
-            cols = pl.ds(c * M, M)
+        for p in range(2):
+            cols = pl.ds(p * M, M)
             a = dot(xs[h], uh[:, cols])
-            p = a[:H] + a[H:] + dot(xs[h, pl.ds(0, H), :], ul[:, cols])
+            x = a[:H] + a[H:] + dot(xs[h, pl.ds(0, H), :], ul[:, cols])
             for i in range(4):
-                block = p[:, i * B:(i + 1) * B]
+                block = x[:, i * B:(i + 1) * B]
                 turned = pltpu.roll(block, H, 1)
-                sw[h * 2, c * 4 + i] = jnp.where(left, block[:Q], turned[Q:])
-                sw[h * 2 + 1, c * 4 + i] = jnp.where(left, turned[:Q], block[Q:])
-            for n in ((h, 0, c), (h, 1, c)) if h == 0 else ((h, 0, c),):
-                w_start(*n, first)
-        if h:
+                sw[h * 2 + p, 2 * i] = jnp.where(left, block[:Q], turned[Q:])
+                sw[h * 2 + p, 2 * i + 1] = jnp.where(left, turned[:Q], block[Q:])
             for c in range(2):
-                w_start(h, 1, c, first)
-        for p in range(2):
+                w_start(h, p, c, first)
             if first:
                 w[h * 2 + p, mine, keep] = sw[h * 2 + p, mine, keep]
             else:
@@ -317,7 +315,22 @@
                 unless_mine(chip, c, z_copy(h, p, mine, chip, c).start)
         z_in[h * 2 + p, mine] = sz[h * 2 + p, mine]
 
+    def hear():
+        pl.semaphore_wait(up_sem, 1)
+        pl.semaphore_wait(down_sem, 1)
+
+    def pass_word(k, place):
+        @pl.when(k < 3)
+        def _():
+            if place:
+                hear()
+            else:
+                pl.when(k > 0)(hear)
+            pl.semaphore_signal(up_sem, inc=1, device_id=(nxt, me), device_id_type=MESH)
+            pl.semaphore_signal(down_sem, inc=1, device_id=(prv, me), device_id_type=MESH)
+
     def turn(k, carry):
+        pass_word(k, 0)
         def waits(h, p, c):
             pl.when(k == 0)(lambda: wait_w(h, p, c, True))
             pl.when(k > 0)(lambda: wait_w(h, p, c, False))
@@ -348,7 +361,11 @@
             waits(0, p, 1)
             lacc[p] = left_part(0, pl.ds(0, M), left_rows(0, p, 0) + left_rows(0, p, 1))
         finish(0)
-        pl.when(k == 3)(lambda: send_residual(0))
+        @pl.when(k == 3)
+        def _():
+            hear()
+            send_residual(0)
+
         pl.when(k != 3)(lambda: left_inverse(0, 0))
         finish(1)
 
@@ -365,6 +382,7 @@
         left_inverse(1, 0)
         left_inverse(1, 1)
 
+        pass_word(k, 1)
         pl.when(k == 0)(lambda: wait_w_sent(True))
         pl.when(k > 0)(lambda: wait_w_sent(False))
 
@@ -374,6 +392,8 @@
             coef_shift.start()
 
         for h in range(2):
+            if h:
+                pass_word(k, 2)
             rows = rows_of(h)
             for p in range(2):
                 for c in range(2):
@@ -471,7 +491,7 @@
             dma((4,)), dma((5,)), four, four, four, four, four, four,
             two, two, dma, dma, two, two,
             eight, eight, eight, eight, eight, eight,
-            sixteen, sixteen, sixteen, sixteen,
+            sixteen, sixteen, sixteen, sixteen, pltpu.SemaphoreType.REGULAR, pltpu.SemaphoreType.REGULAR,
         ],
         compiler_params=pltpu.CompilerParams(
             collective_id=0, has_side_effects=True, vmem_limit_bytes=55000000

time: 113 us -> 112 us (level)
  no operation moved by 1% of the time
where the time goes in v7:
time: 112 us; the launch traced here: 111 us
  Pallas kernels  108 us (96%)
  local copies, waits for them, and re-layouts  2.27 us (2%)
    pallas_call x1, Pallas kernels, on_device(): pl.pallas_call(kernel, out_shape=(jax.ShapeDtypeStruct((B, N), F32), jax....  108 us
    unnamed x4, local copies, waits for them, and re-layouts  2.27 us

profile of v7, /device:TPU:1, one launch (start us, length us, event | category | flops | bytes accessed | tf_op | source)
XLA Modules:
  0.0 111.4 jit_solution(11720316737500776424)
XLA Ops:
  0.6 0.0 copy-start
  0.6 0.7 copy-done
  1.3 108.5 %mgrit_cycle.1 = (f32[128,1024]{1,0:T(8,128)S(1)}, f32[128,1024]{1,0:T(8,128)S(1)}) custom-call(f32[128,1024]{1,0:T(8,128)} %init_h.1, f32[128,1024]{1,0:T(8,128)} %bitcast.9, f32[128,1024]{1,0:T(8,128)} %bitcast.10, f32[128,1024]{1,0:T(8,128)} %bitcast.11, f32[1024,1024]{1,0:T(8,128)} %u_h.1, f32[1,1024]{1,0:T(1,128)S(1)} %bitcast.8, f32[1024,1024]{1,0:T(8,128)} %carried_h.1), custom_call_target="tpu_custom_call" | custom-call | tf_op jit(solution)/shard_map/mgrit_cycle/pallas_call | solution.py:478
  109.8 0.8 copy.11
  110.6 0.8 copy.12
Async XLA Ops:
  0.6 0.7 copy-start
